TPU v7x, 32 devices: a whole 2x2x4 slice. The times are simulated.
32 devices in a mesh: layer: 4 (over x, core), harm: 8 (over z, y).
Axes of the slice: x: 2, y: 2, z: 4, core: 2. Of those that a mesh axis runs over, the one named last changes fastest.
Arguments:
- source: bfloat16 [2, 2048, 128], P(None, 'harm'), may hold values from -6 to 6
- transfer: bfloat16 [4, 2, 2048, 2048], P('layer', None, 'harm'), may hold values from -0.09375 to 0.09375
- fields: bfloat16 [4, 2, 2048, 128], P('layer', None, 'harm'), may hold values from -6 to 6
- orders: int32 [2048], replicated, may hold values from 0 to 2047, each once
Outputs:
- gradients: float32 [4, 2, 4096], P('layer', None, 'harm')
- boundary: bfloat16 [4, 2, 2048, 128], P('layer', None, 'harm')
Inputs may be any that keep to these rules, and one draw needn't show every extreme that they name: `orders`: every value from 0 to 2047 appears exactly once.
All inputs are finite; a program needn't handle non-finite values.
Results may differ from a plain program's by a relative error of at most 0.006.
Values may be sent and summed in bfloat16 or wider, within the bound.
No kernel may reach another device: no remote copies, remote signals or barrier semaphores. Data moves between devices by JAX's collectives and lax.ppermute only.
A program may use at most 64 MiB of HBM per device.

v0:
```python
import math

import jax
import jax.numpy as jnp
from jax import lax
from jax.experimental import pallas as pl
from jax.experimental.pallas import tpu as pltpu
from jax.sharding import PartitionSpec as P


LANES = 128
VMEM = pltpu.VMEM
BF16 = jnp.bfloat16
F32 = jnp.float32


def call(body, outs, args, limit, scratch=()):
    spec = pl.BlockSpec(memory_space=VMEM)
    return pl.pallas_call(
        body,
        out_shape=outs,
        in_specs=[spec] * len(args),
        out_specs=jax.tree.map(lambda _: spec, outs),
        scratch_shapes=list(scratch),
        compiler_params=pltpu.CompilerParams(vmem_limit_bytes=limit << 20),
    )(*[pltpu.with_memory_space_constraint(a, VMEM) for a in args])


def joined(value):
    return jnp.concatenate([value[0], value[1]], axis=1)


QUARTERS = {
    "far": (3, 2, 1, 0),
    "out": (1, 3, 0, 2),
    "in": (2, 0, 3, 1),
    "own": (0, 1, 2, 3),
}
ORDER = ("far0", "own1", "far1", "out0", "out1", "in0", "in1", "own0")


def routes(count):
    if count == len(ORDER):
        return [
            [QUARTERS[slot[:-1]][h // 2] * 2 + (h % 2 ^ int(slot[-1])) for h in range(count)]
            for slot in ORDER
        ]
    return [[(h + s) % count for h in range(count)] for s in range(count - 1, -1, -1)]


def partner(step, fan):
    if not fan:
        return 0
    targets = routes(lax.axis_size("harm"))[step]
    here = lax.axis_index("harm")
    origin = jnp.int32(targets.index(0))
    for spot in range(1, len(targets)):
        origin = jnp.where(here == spot, targets.index(spot), origin)
    return origin


def product(matrix_ref, shards, fan):
    rows = matrix_ref.shape[1]
    part = jnp.zeros((rows, 2 * LANES), F32)
    by_re, by_im = part, part
    for step, value in enumerate(shards):
        size = value.shape[1]
        start = pl.multiple_of(partner(step, fan) * size, size) if fan else 0
        cols = pl.ds(start, size)
        both = joined(value)
        by_re += jnp.dot(matrix_ref[0, :, cols], both, preferred_element_type=F32)
        by_im += jnp.dot(matrix_ref[1, :, cols], both, preferred_element_type=F32)
    re = by_re[:, :LANES] - by_im[:, LANES:]
    im = by_re[:, LANES:] + by_im[:, :LANES]
    return re.astype(BF16), im.astype(BF16)


def propagate(matrix, shards, fan):
    def body(matrix_ref, *refs):
        out_ref = refs[-1]
        re, im = product(matrix_ref, [r[...] for r in refs[:-1]], fan)
        out_ref[0] = re
        out_ref[1] = im

    rows = matrix.shape[1]
    return call(body, VMEM((2, rows, LANES), BF16), [matrix, *shards], 8)


def one_hot(targets, first, count):
    index = lax.broadcasted_iota(jnp.int32, (count, targets.shape[1]), 0) + first
    return jnp.where(index == targets, 1.0, 0.0).astype(BF16)


def bring(matrix, source, orders):
    args = [matrix, source, orders]

    def body(*refs):
        size = len(args)
        ins, outs, sems = refs[:size], refs[size : 2 * size], refs[-1]
        copies = [
            pltpu.make_async_copy(ins[i], outs[i], sems.at[i]) for i in range(size)
        ]
        for copy in copies:
            copy.start()
        for copy in copies:
            copy.wait()

    hbm = pl.BlockSpec(memory_space=pltpu.HBM)
    return pl.pallas_call(
        body,
        out_shape=[VMEM(a.shape, a.dtype) for a in args],
        in_specs=[hbm] * len(args),
        out_specs=[pl.BlockSpec(memory_space=VMEM)] * len(args),
        scratch_shapes=[pltpu.SemaphoreType.DMA((len(args),))],
        compiler_params=pltpu.CompilerParams(vmem_limit_bytes=1 << 20),
        name="bring",
    )(*[pltpu.with_memory_space_constraint(a, pltpu.HBM) for a in args])


def sort_fields(orders, groups, fan, split):
    harmonics = orders.shape[1]
    blocks = harmonics // LANES
    pieces = len(groups[0])

    def body(orders_ref, *refs):
        shard_refs, out_ref, whole = refs[:-2], refs[-2], refs[-1]
        values = [r[...] for r in shard_refs[:pieces]]
        if len(groups) > 1:
            low = lax.axis_index("layer") < split
            values = [
                jnp.where(low, v, r[...]) for v, r in zip(values, shard_refs[pieces:])
            ]
        fill(whole, values, fan)
        targets = orders_ref[...] ^ (LANES - 1)
        chunk = 4 * LANES

        def step(c, carry):
            picked = jnp.dot(
                one_hot(targets, c * chunk, chunk), whole[...], preferred_element_type=F32
            ).astype(BF16)
            for b in range(chunk // LANES):
                re = picked[b * LANES : (b + 1) * LANES, :LANES]
                im = picked[b * LANES : (b + 1) * LANES, LANES:]
                at = pl.multiple_of((c * (chunk // LANES) + b) * 2 * LANES, LANES)
                out_ref[:LANES, pl.ds(at, LANES)] = re
                out_ref[:LANES, pl.ds(at + LANES, LANES)] = -im
                out_ref[LANES:, pl.ds(at, LANES)] = im
                out_ref[LANES:, pl.ds(at + LANES, LANES)] = re
            return carry

        lax.fori_loop(0, harmonics // chunk, step, 0)

    return call(
        body,
        VMEM((2 * LANES, blocks * 2 * LANES), BF16),
        [orders, *[a for group in groups for a in group]],
        24,
        [VMEM((harmonics, 2 * LANES), BF16)],
    )


def fill(whole, shards, fan):
    for step, value in enumerate(shards):
        size = value.shape[1]
        start = pl.multiple_of(partner(step, fan) * size, size) if fan else 0
        whole[pl.ds(start, size), :LANES] = value[0]
        whole[pl.ds(start, size), LANES:] = value[1]


def finish(matrix, orders, factors, sets, belows, fan, band, scale):
    layers = len(sets)
    harmonics = orders.shape[1]
    rows = matrix.shape[1]
    blocks = harmonics // LANES
    bands = band // LANES
    strip = bands + 1
    per_set = [len(s) for s in sets]

    def body(matrix_ref, orders_ref, factors_ref, *refs):
        refs = list(refs)
        set_refs = []
        for count in per_set:
            set_refs.append(refs[:count])
            refs = refs[count:]
        below_refs, refs = refs[: layers - 1], refs[layers - 1 :]
        grad_ref, bottom_ref, whole, moved = refs
        layer = lax.axis_index("layer")
        last = [r[...] for r in set_refs[0]]
        chosen = last
        for index in range(1, layers):
            chosen = [
                jnp.where(layer == index, r[...], c) for r, c in zip(set_refs[index], chosen)
            ]
        fill(whole, chosen, fan)
        re, im = product(matrix_ref, last, fan)
        for index in range(1, layers):
            re = jnp.where(layer == index, below_refs[index - 1][0], re)
            im = jnp.where(layer == index, below_refs[index - 1][1], im)
        bottom_ref[0, 0] = re
        bottom_ref[0, 1] = im

        targets = orders_ref[...] + (harmonics - 1 - band * lax.axis_index("harm"))
        for c in range(blocks + bands):
            picked = jnp.dot(
                one_hot(targets, c * LANES, LANES), whole[...], preferred_element_type=F32
            ).astype(BF16)
            moved[:, c * 2 * LANES : (c + 1) * 2 * LANES] = picked
        width = 2 * LANES
        length = blocks * width
        parts = []
        for q in range(strip):
            parts.append(
                lax.dot_general(
                    factors_ref[...],
                    moved[:, q * width : q * width + length],
                    (((1,), (1,)), ((), ())),
                    preferred_element_type=F32,
                )
            )
        strips = jnp.concatenate(parts, axis=1)
        size = strip * LANES
        for part in range(2):
            skewed = pltpu.roll(
                strips[part * LANES : (part + 1) * LANES],
                size - (LANES - 1),
                1,
                stride=1,
                stride_axis=0,
            )
            total = jnp.sum(skewed[:, :band], axis=0, keepdims=True) * scale
            grad_ref[0, pl.ds(part, 1), :] = total

    outs = (
        jax.ShapeDtypeStruct((1, 2, band), F32),
        jax.ShapeDtypeStruct((1, 2, rows, LANES), BF16),
    )
    args = [matrix, orders, factors]
    for group in sets:
        args += group
    args += belows
    return call(
        body,
        outs,
        args,
        24,
        [
            VMEM((harmonics, 2 * LANES), BF16),
            VMEM((LANES, (blocks + bands) * 2 * LANES), BF16),
        ],
    )


def sweep_layers(source, transfer, fields, orders):
    layers = lax.axis_size("layer")
    count = lax.axis_size("harm")
    harmonics = orders.shape[0]
    columns = source.shape[2]
    rows = source.shape[1]
    fan = rows % LANES == 0 and layers > 3
    band = 2 * harmonics // count
    scale = 1.0 / math.sqrt(harmonics * columns)
    axes = ("layer", "harm")
    top = layers - 1
    plan = routes(count) if fan else []
    still = list(range(count))

    def gathered(value):
        return [lax.all_gather(value, "harm", axis=1, tiled=True)]

    def to_layer(value, origins, target):
        if not fan:
            if origins[0] != target:
                pairs = [(origins[0] * count + h, target * count + h) for h in range(count)]
                value = lax.ppermute(value, axes, pairs)
            return gathered(value)
        out = []
        for origin, route in zip(origins, plan):
            if origin == target and route == still:
                out.append(value)
                continue
            pairs = [(origin * count + h, target * count + route[h]) for h in range(count)]
            out.append(lax.ppermute(value, axes, pairs))
        return out

    def in_layers(value, members):
        out = []
        for route in plan:
            if route == still:
                out.append(value)
                continue
            pairs = [(r * count + h, r * count + route[h]) for r in members for h in range(count)]
            out.append(lax.ppermute(value, axes, pairs))
        return out

    matrix, own, table = bring(transfer[0], source, orders.reshape(1, harmonics))
    if fan:
        origins = [(s + 1) % (layers - 1) for s in range(count - 1)] + [top]
    else:
        origins = [top]
    shards = to_layer(source, origins, top)
    if fan:
        shards[-1] = own
    sets = [shards]
    belows = []
    early = tuple(r for r in range(layers) if r < layers // 2)
    late = tuple(r for r in range(layers) if r >= layers // 2)
    mine = []
    for layer in range(top, 0, -1):
        below = propagate(matrix, shards, fan)
        belows.append(below)
        shards = to_layer(below, [layer] * count, layer - 1)
        sets.append(shards)
        if fan and layer > top - 2:
            held, _ = lax.optimization_barrier((fields[0], below))
            mine.append(in_layers(held, early if layer == top else late))
    if not fan:
        mine = [gathered(fields[0])]
    factors = sort_fields(table, mine, fan, len(early))
    grads, bottom = finish(
        matrix, table, factors, sets[::-1], belows[::-1], fan, band, scale
    )
    return grads, bottom


def solution(mesh):
    return jax.shard_map(
        sweep_layers,
        mesh=mesh,
        in_specs=(
            P(None, "harm", None),
            P("layer", None, "harm", None),
            P("layer", None, "harm", None),
            P(),
        ),
        out_specs=(P("layer", None, "harm"), P("layer", None, "harm", None)),
        check_vma=False,
    )
```

profile of v0, /device:TPU:0, one launch (start us, length us, event | category | flops | bytes accessed | tf_op | source)
XLA Modules:
  0.0 156.4 jit_solution(11758967020712923779)
XLA Ops:
  2.0 9.6 %collective-permute-start.2 = (bf16[2,256,128]{2,1,0:T(8,128)(2,1)}, bf16[2,256,128]{2,1,0:T(8,128)(2,1)S(1)}, u32[]{:S(2)}, u32[]{:S(2)}) collective-permute-start(bf16[2,256,128]{2,1,0:T(8,128)(2,1)} %refs_1_.1), channel_id=1, source_target_pairs={{0,31},{1,30},{2,29},{3,28},{4,27},{5,26},{6,25},{7,24}} | collective-permute-start | bytes 393224 | tf_op jit(solution)/shard_map/ppermute | solution.py:282
  12.9 1.3 collective-permute-start.5
  14.9 1.6 %bring.1 = (bf16[2,256,2048]{2,1,0:T(8,128)(2,1)S(1)}, bf16[2,256,128]{2,1,0:T(8,128)(2,1)S(1)}, s32[1,2048]{1,0:T(1,128)S(1)}) custom-call(bf16[2,256,2048]{2,1,0:T(8,128)(2,1)} %bitcast.19, bf16[2,256,128]{2,1,0:T(8,128)(2,1)} %refs_1_.1, s32[1,2048]{1,0:T(1,128)} %bitcast.20), custom_call_target="tpu_custom_call" | custom-call | tf_op jit(solution)/shard_map/bring/pallas_call | solution.py:109
  17.9 9.0 %collective-permute-start.7 = (bf16[2,256,128]{2,1,0:T(8,128)(2,1)S(1)}, bf16[2,256,128]{2,1,0:T(8,128)(2,1)S(1)}, u32[]{:S(2)}, u32[]{:S(2)}) collective-permute-start(bf16[2,256,128]{2,1,0:T(8,128)(2,1)S(1)} %bitcast.3), channel_id=1, source_target_pairs={{0,6},{1,7},{2,4},{3,5},{4,2},{5,3},{6,0},{7,1},{8,14},{9,15},{10,... | collective-permute-start | bytes 393224 | tf_op jit(solution)/shard_map/ppermute | solution.py:292
  29.5 4.9 %collective-permute-done.7.refs_0_ = bf16[2,256,128]{2,1,0:T(8,128)(2,1)S(1)} collective-permute-done((bf16[2,256,128]{2,1,0:T(8,128)(2,1)S(1)}, bf16[2,256,128]{2,1,0:T(8,128)(2,1)S(1)}, u32[]{:S(2)}, u32[]{:S(2)}) %collective-permute-start.7) | collective-permute-done | bytes 131104 | tf_op jit(solution)/shard_map/ppermute | solution.py:292
  37.2 3.4 %collective-permute-start.8 = (bf16[2,256,128]{2,1,0:T(8,128)(2,1)S(1)}, bf16[2,256,128]{2,1,0:T(8,128)(2,1)S(1)}, u32[]{:S(2)}, u32[]{:S(2)}) collective-permute-start(bf16[2,256,128]{2,1,0:T(8,128)(2,1)S(1)} %bitcast.4), channel_id=1, source_target_pairs={{0,1},{1,0},{2,3},{3,2},{4,5},{5,4},{6,7},{7,6},{8,9},{9,8},{10,11... | collective-permute-start | bytes 393224 | tf_op jit(solution)/shard_map/ppermute | solution.py:292
  40.6 9.1 %collective-permute-start.9 = (bf16[2,256,128]{2,1,0:T(8,128)(2,1)S(1)}, bf16[2,256,128]{2,1,0:T(8,128)(2,1)S(1)}, u32[]{:S(2)}, u32[]{:S(2)}) collective-permute-start(bf16[2,256,128]{2,1,0:T(8,128)(2,1)S(1)} %bitcast.5), channel_id=1, source_target_pairs={{0,7},{1,6},{2,5},{3,4},{4,3},{5,2},{6,1},{7,0},{8,15},{9,14},{10,... | collective-permute-start | bytes 393224 | tf_op jit(solution)/shard_map/ppermute | solution.py:292
  49.7 3.8 %collective-permute-start.10 = (bf16[2,256,128]{2,1,0:T(8,128)(2,1)S(1)}, bf16[2,256,128]{2,1,0:T(8,128)(2,1)S(1)}, u32[]{:S(2)}, u32[]{:S(2)}) collective-permute-start(bf16[2,256,128]{2,1,0:T(8,128)(2,1)S(1)} %bitcast.6), channel_id=1, source_target_pairs={{0,2},{1,3},{2,6},{3,7},{4,0},{5,1},{6,4},{7,5},{8,10},{9,11},{10,... | collective-permute-start | bytes 393224 | tf_op jit(solution)/shard_map/ppermute | solution.py:292
  53.5 5.3 %collective-permute-start.11 = (bf16[2,256,128]{2,1,0:T(8,128)(2,1)S(1)}, bf16[2,256,128]{2,1,0:T(8,128)(2,1)S(1)}, u32[]{:S(2)}, u32[]{:S(2)}) collective-permute-start(bf16[2,256,128]{2,1,0:T(8,128)(2,1)S(1)} %bitcast.7), channel_id=1, source_target_pairs={{0,3},{1,2},{2,7},{3,6},{4,1},{5,0},{6,5},{7,4},{8,11},{9,10},{10,... | collective-permute-start | bytes 393224 | tf_op jit(solution)/shard_map/ppermute | solution.py:292
  58.8 2.4 %collective-permute-start.12 = (bf16[2,256,128]{2,1,0:T(8,128)(2,1)S(1)}, bf16[2,256,128]{2,1,0:T(8,128)(2,1)S(1)}, u32[]{:S(2)}, u32[]{:S(2)}) collective-permute-start(bf16[2,256,128]{2,1,0:T(8,128)(2,1)S(1)} %bitcast.8), channel_id=1, source_target_pairs={{0,4},{1,5},{2,0},{3,1},{4,6},{5,7},{6,2},{7,3},{8,12},{9,13},{10,... | collective-permute-start | bytes 393224 | tf_op jit(solution)/shard_map/ppermute | solution.py:292
  61.9 2.0 %collective-permute-start.13 = (bf16[2,256,128]{2,1,0:T(8,128)(2,1)S(1)}, bf16[2,256,128]{2,1,0:T(8,128)(2,1)S(1)}, u32[]{:S(2)}, u32[]{:S(2)}) collective-permute-start(bf16[2,256,128]{2,1,0:T(8,128)(2,1)S(1)} %bitcast.9), channel_id=1, source_target_pairs={{0,5},{1,4},{2,1},{3,0},{4,7},{5,6},{6,3},{7,2},{8,13},{9,12},{10,... | collective-permute-start | bytes 393224 | tf_op jit(solution)/shard_map/ppermute | solution.py:292
  65.4 3.2 %collective-permute-done.11.refs_4_ = bf16[2,256,128]{2,1,0:T(8,128)(2,1)S(1)} collective-permute-done((bf16[2,256,128]{2,1,0:T(8,128)(2,1)S(1)}, bf16[2,256,128]{2,1,0:T(8,128)(2,1)S(1)}, u32[]{:S(2)}, u32[]{:S(2)}) %collective-permute-start.11) | collective-permute-done | bytes 131104 | tf_op jit(solution)/shard_map/ppermute | solution.py:292
  69.9 1.4 collective-permute-done.13.refs_6_
  74.0 12.6 %collective-permute-start.22 = (bf16[2,256,128]{2,1,0:T(8,128)(2,1)S(1)}, bf16[2,256,128]{2,1,0:T(8,128)(2,1)S(1)}, u32[]{:S(2)}, u32[]{:S(2)}) collective-permute-start(bf16[2,256,128]{2,1,0:T(8,128)(2,1)S(1)} %bitcast.10), channel_id=1, source_target_pairs={{16,22},{17,23},{18,20},{19,21},{20,18},{21,19},{22,16},{23,17},{2... | collective-permute-start | bytes 393224 | tf_op jit(solution)/shard_map/ppermute | solution.py:292
  86.6 7.0 %collective-permute-start.23 = (bf16[2,256,128]{2,1,0:T(8,128)(2,1)S(1)}, bf16[2,256,128]{2,1,0:T(8,128)(2,1)S(1)}, u32[]{:S(2)}, u32[]{:S(2)}) collective-permute-start(bf16[2,256,128]{2,1,0:T(8,128)(2,1)S(1)} %bitcast.11), channel_id=1, source_target_pairs={{16,17},{17,16},{18,19},{19,18},{20,21},{21,20},{22,23},{23,22},{2... | collective-permute-start | bytes 393224 | tf_op jit(solution)/shard_map/ppermute | solution.py:292
  93.6 7.0 %collective-permute-start.24 = (bf16[2,256,128]{2,1,0:T(8,128)(2,1)S(1)}, bf16[2,256,128]{2,1,0:T(8,128)(2,1)S(1)}, u32[]{:S(2)}, u32[]{:S(2)}) collective-permute-start(bf16[2,256,128]{2,1,0:T(8,128)(2,1)S(1)} %bitcast.12), channel_id=1, source_target_pairs={{16,23},{17,22},{18,21},{19,20},{20,19},{21,18},{22,17},{23,16},{2... | collective-permute-start | bytes 393224 | tf_op jit(solution)/shard_map/ppermute | solution.py:292
  100.6 7.0 %collective-permute-start.25 = (bf16[2,256,128]{2,1,0:T(8,128)(2,1)S(1)}, bf16[2,256,128]{2,1,0:T(8,128)(2,1)S(1)}, u32[]{:S(2)}, u32[]{:S(2)}) collective-permute-start(bf16[2,256,128]{2,1,0:T(8,128)(2,1)S(1)} %bitcast.13), channel_id=1, source_target_pairs={{16,18},{17,19},{18,22},{19,23},{20,16},{21,17},{22,20},{23,21},{2... | collective-permute-start | bytes 393224 | tf_op jit(solution)/shard_map/ppermute | solution.py:292
  107.6 7.0 %collective-permute-start.26 = (bf16[2,256,128]{2,1,0:T(8,128)(2,1)S(1)}, bf16[2,256,128]{2,1,0:T(8,128)(2,1)S(1)}, u32[]{:S(2)}, u32[]{:S(2)}) collective-permute-start(bf16[2,256,128]{2,1,0:T(8,128)(2,1)S(1)} %bitcast.14), channel_id=1, source_target_pairs={{16,19},{17,18},{18,23},{19,22},{20,17},{21,16},{22,21},{23,20},{2... | collective-permute-start | bytes 393224 | tf_op jit(solution)/shard_map/ppermute | solution.py:292
  115.4 7.0 %collective-permute-start.27 = (bf16[2,256,128]{2,1,0:T(8,128)(2,1)S(1)}, bf16[2,256,128]{2,1,0:T(8,128)(2,1)S(1)}, u32[]{:S(2)}, u32[]{:S(2)}) collective-permute-start(bf16[2,256,128]{2,1,0:T(8,128)(2,1)S(1)} %bitcast.15), channel_id=1, source_target_pairs={{16,20},{17,21},{18,16},{19,17},{20,22},{21,23},{22,18},{23,19},{2... | collective-permute-start | bytes 393224 | tf_op jit(solution)/shard_map/ppermute | solution.py:292
  122.4 7.0 %collective-permute-start.28 = (bf16[2,256,128]{2,1,0:T(8,128)(2,1)S(1)}, bf16[2,256,128]{2,1,0:T(8,128)(2,1)S(1)}, u32[]{:S(2)}, u32[]{:S(2)}) collective-permute-start(bf16[2,256,128]{2,1,0:T(8,128)(2,1)S(1)} %bitcast.16), channel_id=1, source_target_pairs={{16,21},{17,20},{18,17},{19,16},{20,23},{21,22},{22,19},{23,18},{2... | collective-permute-start | bytes 393224 | tf_op jit(solution)/shard_map/ppermute | solution.py:292
  136.0 1.6 %collective-permute-done.37.refs_0_ = bf16[2,256,128]{2,1,0:T(8,128)(2,1)S(1)} collective-permute-done((bf16[2,256,128]{2,1,0:T(8,128)(2,1)S(1)}, bf16[2,256,128]{2,1,0:T(8,128)(2,1)S(1)}, u32[]{:S(2)}, u32[]{:S(2)}) %collective-permute-start.37) | collective-permute-done | bytes 131104 | tf_op jit(solution)/shard_map/ppermute | solution.py:282
  138.9 2.7 %collective-permute-done.38.refs_1_ = bf16[2,256,128]{2,1,0:T(8,128)(2,1)S(1)} collective-permute-done((bf16[2,256,128]{2,1,0:T(8,128)(2,1)S(1)}, bf16[2,256,128]{2,1,0:T(8,128)(2,1)S(1)}, u32[]{:S(2)}, u32[]{:S(2)}) %collective-permute-start.38) | collective-permute-done | bytes 131104 | tf_op jit(solution)/shard_map/ppermute | solution.py:282
  144.3 3.3 %shard_map.61.factors_ref = bf16[256,4096]{1,0:T(8,128)(2,1)S(1)} custom-call(s32[1,2048]{1,0:T(1,128)S(1)} %get-tuple-element.8.orders_ref, bf16[2,256,128]{2,1,0:T(8,128)(2,1)S(1)} %collective-permute-done.7.refs_0_, bf16[2,256,128]{2,1,0:T(8,128)(2,1)S(1)} %collective-permute-done.8.refs_1_, bf16[2,256,128]{2,1,0:T(8,128)(2,1)S(1)} %collective-permute-done.9.refs_2_, ...), custom_call_target="tpu_custom_call" | custom-call | tf_op jit(solution)/shard_map/pallas_call | solution.py:19
  148.8 7.5 %shard_map.63 = (f32[1,2,512]{2,1,0:T(2,128)}, bf16[1,2,256,128]{3,2,1,0:T(8,128)(2,1)}) custom-call(bf16[2,256,2048]{2,1,0:T(8,128)(2,1)S(1)} %get-tuple-element.7.matrix_ref, s32[1,2048]{1,0:T(1,128)S(1)} %get-tuple-element.8.orders_ref, bf16[256,4096]{1,0:T(8,128)(2,1)S(1)} %shard_map.61.factors_ref, ...), custom_call_target="tpu_custom_call" | custom-call | tf_op jit(solution)/shard_map/pallas_call | solution.py:19
  (74 shorter events, 28.4 us)
Async XLA Ops:
  0.6 12.3 %collective-permute-start = (bf16[2,256,128]{2,1,0:T(8,128)(2,1)}, bf16[2,256,128]{2,1,0:T(8,128)(2,1)S(1)}, u32[]{:S(2)}, u32[]{:S(2)}) collective-permute-start(bf16[2,256,128]{2,1,0:T(8,128)(2,1)} %refs_1_.1), channel_id=1, source_target_pairs={{8,30},{9,31},{10,28},{11,29},{12,26},{13,27},{14,24},{15,25}} | collective-permute-start | bytes 393224 | tf_op jit(solution)/shard_map/ppermute | solution.py:282
  1.3 12.9 %collective-permute-start.1 = (bf16[2,256,128]{2,1,0:T(8,128)(2,1)}, bf16[2,256,128]{2,1,0:T(8,128)(2,1)S(1)}, u32[]{:S(2)}, u32[]{:S(2)}) collective-permute-start(bf16[2,256,128]{2,1,0:T(8,128)(2,1)} %refs_1_.1), channel_id=1, source_target_pairs={{16,25},{17,24},{18,27},{19,26},{20,29},{21,28},{22,31},{23,30}} | collective-permute-start | bytes 393224 | tf_op jit(solution)/shard_map/ppermute | solution.py:282
  2.0 14.6 %collective-permute-start.2 = (bf16[2,256,128]{2,1,0:T(8,128)(2,1)}, bf16[2,256,128]{2,1,0:T(8,128)(2,1)S(1)}, u32[]{:S(2)}, u32[]{:S(2)}) collective-permute-start(bf16[2,256,128]{2,1,0:T(8,128)(2,1)} %refs_1_.1), channel_id=1, source_target_pairs={{0,31},{1,30},{2,29},{3,28},{4,27},{5,26},{6,25},{7,24}} | collective-permute-start | bytes 393224 | tf_op jit(solution)/shard_map/ppermute | solution.py:282
  17.9 16.6 %collective-permute-start.7 = (bf16[2,256,128]{2,1,0:T(8,128)(2,1)S(1)}, bf16[2,256,128]{2,1,0:T(8,128)(2,1)S(1)}, u32[]{:S(2)}, u32[]{:S(2)}) collective-permute-start(bf16[2,256,128]{2,1,0:T(8,128)(2,1)S(1)} %bitcast.3), channel_id=1, source_target_pairs={{0,6},{1,7},{2,4},{3,5},{4,2},{5,3},{6,0},{7,1},{8,14},{9,15},{10,... | collective-permute-start | bytes 393224 | tf_op jit(solution)/shard_map/ppermute | solution.py:292
  35.1 14.6 %collective-permute-start.19 = (bf16[2,256,128]{2,1,0:T(8,128)(2,1)S(1)}, bf16[2,256,128]{2,1,0:T(8,128)(2,1)S(1)}, u32[]{:S(2)}, u32[]{:S(2)}) collective-permute-start(bf16[2,256,128]{2,1,0:T(8,128)(2,1)S(1)} %shard_map.59.refs_34_), channel_id=1, source_target_pairs={{24,20},{25,21},{26,16},{27,17},{28,22},{29,23},{30,18},{31,19}} | collective-permute-start | bytes 393224 | tf_op jit(solution)/shard_map/ppermute | solution.py:282
  35.8 17.7 %collective-permute-start.20 = (bf16[2,256,128]{2,1,0:T(8,128)(2,1)S(1)}, bf16[2,256,128]{2,1,0:T(8,128)(2,1)S(1)}, u32[]{:S(2)}, u32[]{:S(2)}) collective-permute-start(bf16[2,256,128]{2,1,0:T(8,128)(2,1)S(1)} %shard_map.59.refs_34_), channel_id=1, source_target_pairs={{24,21},{25,20},{26,17},{27,16},{28,23},{29,22},{30,19},{31,18}} | collective-permute-start | bytes 393224 | tf_op jit(solution)/shard_map/ppermute | solution.py:282
  36.5 22.3 %collective-permute-start.21 = (bf16[2,256,128]{2,1,0:T(8,128)(2,1)S(1)}, bf16[2,256,128]{2,1,0:T(8,128)(2,1)S(1)}, u32[]{:S(2)}, u32[]{:S(2)}) collective-permute-start(bf16[2,256,128]{2,1,0:T(8,128)(2,1)S(1)} %shard_map.59.refs_34_), channel_id=1, source_target_pairs={{24,16},{25,17},{26,18},{27,19},{28,20},{29,21},{30,22},{31,23}} | collective-permute-start | bytes 393224 | tf_op jit(solution)/shard_map/ppermute | solution.py:282
  37.2 24.8 %collective-permute-start.8 = (bf16[2,256,128]{2,1,0:T(8,128)(2,1)S(1)}, bf16[2,256,128]{2,1,0:T(8,128)(2,1)S(1)}, u32[]{:S(2)}, u32[]{:S(2)}) collective-permute-start(bf16[2,256,128]{2,1,0:T(8,128)(2,1)S(1)} %bitcast.4), channel_id=1, source_target_pairs={{0,1},{1,0},{2,3},{3,2},{4,5},{5,4},{6,7},{7,6},{8,9},{9,8},{10,11... | collective-permute-start | bytes 393224 | tf_op jit(solution)/shard_map/ppermute | solution.py:292
  40.6 23.4 %collective-permute-start.9 = (bf16[2,256,128]{2,1,0:T(8,128)(2,1)S(1)}, bf16[2,256,128]{2,1,0:T(8,128)(2,1)S(1)}, u32[]{:S(2)}, u32[]{:S(2)}) collective-permute-start(bf16[2,256,128]{2,1,0:T(8,128)(2,1)S(1)} %bitcast.5), channel_id=1, source_target_pairs={{0,7},{1,6},{2,5},{3,4},{4,3},{5,2},{6,1},{7,0},{8,15},{9,14},{10,... | collective-permute-start | bytes 393224 | tf_op jit(solution)/shard_map/ppermute | solution.py:292
  49.7 15.0 %collective-permute-start.10 = (bf16[2,256,128]{2,1,0:T(8,128)(2,1)S(1)}, bf16[2,256,128]{2,1,0:T(8,128)(2,1)S(1)}, u32[]{:S(2)}, u32[]{:S(2)}) collective-permute-start(bf16[2,256,128]{2,1,0:T(8,128)(2,1)S(1)} %bitcast.6), channel_id=1, source_target_pairs={{0,2},{1,3},{2,6},{3,7},{4,0},{5,1},{6,4},{7,5},{8,10},{9,11},{10,... | collective-permute-start | bytes 393224 | tf_op jit(solution)/shard_map/ppermute | solution.py:292
  53.5 15.0 %collective-permute-start.11 = (bf16[2,256,128]{2,1,0:T(8,128)(2,1)S(1)}, bf16[2,256,128]{2,1,0:T(8,128)(2,1)S(1)}, u32[]{:S(2)}, u32[]{:S(2)}) collective-permute-start(bf16[2,256,128]{2,1,0:T(8,128)(2,1)S(1)} %bitcast.7), channel_id=1, source_target_pairs={{0,3},{1,2},{2,7},{3,6},{4,1},{5,0},{6,5},{7,4},{8,11},{9,10},{10,... | collective-permute-start | bytes 393224 | tf_op jit(solution)/shard_map/ppermute | solution.py:292
  71.2 15.3 %collective-permute-start.33 = (bf16[2,256,128]{2,1,0:T(8,128)(2,1)S(1)}, bf16[2,256,128]{2,1,0:T(8,128)(2,1)S(1)}, u32[]{:S(2)}, u32[]{:S(2)}) collective-permute-start(bf16[2,256,128]{2,1,0:T(8,128)(2,1)S(1)} %shard_map.60.refs_33_), channel_id=1, source_target_pairs={{16,11},{17,10},{18,15},{19,14},{20,9},{21,8},{22,13},{23,12}} | collective-permute-start | bytes 393224 | tf_op jit(solution)/shard_map/ppermute | solution.py:282
  71.9 21.7 %collective-permute-start.34 = (bf16[2,256,128]{2,1,0:T(8,128)(2,1)S(1)}, bf16[2,256,128]{2,1,0:T(8,128)(2,1)S(1)}, u32[]{:S(2)}, u32[]{:S(2)}) collective-permute-start(bf16[2,256,128]{2,1,0:T(8,128)(2,1)S(1)} %shard_map.60.refs_33_), channel_id=1, source_target_pairs={{16,12},{17,13},{18,8},{19,9},{20,14},{21,15},{22,10},{23,11}} | collective-permute-start | bytes 393224 | tf_op jit(solution)/shard_map/ppermute | solution.py:282
  72.6 28.0 %collective-permute-start.35 = (bf16[2,256,128]{2,1,0:T(8,128)(2,1)S(1)}, bf16[2,256,128]{2,1,0:T(8,128)(2,1)S(1)}, u32[]{:S(2)}, u32[]{:S(2)}) collective-permute-start(bf16[2,256,128]{2,1,0:T(8,128)(2,1)S(1)} %shard_map.60.refs_33_), channel_id=1, source_target_pairs={{16,13},{17,12},{18,9},{19,8},{20,15},{21,14},{22,11},{23,10}} | collective-permute-start | bytes 393224 | tf_op jit(solution)/shard_map/ppermute | solution.py:282
  73.3 34.3 %collective-permute-start.36 = (bf16[2,256,128]{2,1,0:T(8,128)(2,1)S(1)}, bf16[2,256,128]{2,1,0:T(8,128)(2,1)S(1)}, u32[]{:S(2)}, u32[]{:S(2)}) collective-permute-start(bf16[2,256,128]{2,1,0:T(8,128)(2,1)S(1)} %shard_map.60.refs_33_), channel_id=1, source_target_pairs={{16,8},{17,9},{18,10},{19,11},{20,12},{21,13},{22,14},{23,15}} | collective-permute-start | bytes 393224 | tf_op jit(solution)/shard_map/ppermute | solution.py:282
  74.0 41.4 %collective-permute-start.22 = (bf16[2,256,128]{2,1,0:T(8,128)(2,1)S(1)}, bf16[2,256,128]{2,1,0:T(8,128)(2,1)S(1)}, u32[]{:S(2)}, u32[]{:S(2)}) collective-permute-start(bf16[2,256,128]{2,1,0:T(8,128)(2,1)S(1)} %bitcast.10), channel_id=1, source_target_pairs={{16,22},{17,23},{18,20},{19,21},{20,18},{21,19},{22,16},{23,17},{2... | collective-permute-start | bytes 393224 | tf_op jit(solution)/shard_map/ppermute | solution.py:292
  86.6 35.9 %collective-permute-start.23 = (bf16[2,256,128]{2,1,0:T(8,128)(2,1)S(1)}, bf16[2,256,128]{2,1,0:T(8,128)(2,1)S(1)}, u32[]{:S(2)}, u32[]{:S(2)}) collective-permute-start(bf16[2,256,128]{2,1,0:T(8,128)(2,1)S(1)} %bitcast.11), channel_id=1, source_target_pairs={{16,17},{17,16},{18,19},{19,18},{20,21},{21,20},{22,23},{23,22},{2... | collective-permute-start | bytes 393224 | tf_op jit(solution)/shard_map/ppermute | solution.py:292
  93.6 35.9 %collective-permute-start.24 = (bf16[2,256,128]{2,1,0:T(8,128)(2,1)S(1)}, bf16[2,256,128]{2,1,0:T(8,128)(2,1)S(1)}, u32[]{:S(2)}, u32[]{:S(2)}) collective-permute-start(bf16[2,256,128]{2,1,0:T(8,128)(2,1)S(1)} %bitcast.12), channel_id=1, source_target_pairs={{16,23},{17,22},{18,21},{19,20},{20,19},{21,18},{22,17},{23,16},{2... | collective-permute-start | bytes 393224 | tf_op jit(solution)/shard_map/ppermute | solution.py:292
  100.6 30.1 %collective-permute-start.25 = (bf16[2,256,128]{2,1,0:T(8,128)(2,1)S(1)}, bf16[2,256,128]{2,1,0:T(8,128)(2,1)S(1)}, u32[]{:S(2)}, u32[]{:S(2)}) collective-permute-start(bf16[2,256,128]{2,1,0:T(8,128)(2,1)S(1)} %bitcast.13), channel_id=1, source_target_pairs={{16,18},{17,19},{18,22},{19,23},{20,16},{21,17},{22,20},{23,21},{2... | collective-permute-start | bytes 393224 | tf_op jit(solution)/shard_map/ppermute | solution.py:292
  107.6 24.4 %collective-permute-start.26 = (bf16[2,256,128]{2,1,0:T(8,128)(2,1)S(1)}, bf16[2,256,128]{2,1,0:T(8,128)(2,1)S(1)}, u32[]{:S(2)}, u32[]{:S(2)}) collective-permute-start(bf16[2,256,128]{2,1,0:T(8,128)(2,1)S(1)} %bitcast.14), channel_id=1, source_target_pairs={{16,19},{17,18},{18,23},{19,22},{20,17},{21,16},{22,21},{23,20},{2... | collective-permute-start | bytes 393224 | tf_op jit(solution)/shard_map/ppermute | solution.py:292
  115.4 18.0 %collective-permute-start.27 = (bf16[2,256,128]{2,1,0:T(8,128)(2,1)S(1)}, bf16[2,256,128]{2,1,0:T(8,128)(2,1)S(1)}, u32[]{:S(2)}, u32[]{:S(2)}) collective-permute-start(bf16[2,256,128]{2,1,0:T(8,128)(2,1)S(1)} %bitcast.15), channel_id=1, source_target_pairs={{16,20},{17,21},{18,16},{19,17},{20,22},{21,23},{22,18},{23,19},{2... | collective-permute-start | bytes 393224 | tf_op jit(solution)/shard_map/ppermute | solution.py:292
  122.4 12.3 %collective-permute-start.28 = (bf16[2,256,128]{2,1,0:T(8,128)(2,1)S(1)}, bf16[2,256,128]{2,1,0:T(8,128)(2,1)S(1)}, u32[]{:S(2)}, u32[]{:S(2)}) collective-permute-start(bf16[2,256,128]{2,1,0:T(8,128)(2,1)S(1)} %bitcast.16), channel_id=1, source_target_pairs={{16,21},{17,20},{18,17},{19,16},{20,23},{21,22},{22,19},{23,18},{2... | collective-permute-start | bytes 393224 | tf_op jit(solution)/shard_map/ppermute | solution.py:292
  133.4 14.2 %collective-permute-start.40 = (bf16[2,256,128]{2,1,0:T(8,128)(2,1)S(1)}, bf16[2,256,128]{2,1,0:T(8,128)(2,1)S(1)}, u32[]{:S(2)}, u32[]{:S(2)}) collective-permute-start(bf16[2,256,128]{2,1,0:T(8,128)(2,1)S(1)} %shard_map.62.refs_32_), channel_id=1, source_target_pairs={{8,2},{9,3},{10,6},{11,7},{12,0},{13,1},{14,4},{15,5}} | collective-permute-start | bytes 393224 | tf_op jit(solution)/shard_map/ppermute | solution.py:282
  134.7 12.9 %collective-permute-start.41 = (bf16[2,256,128]{2,1,0:T(8,128)(2,1)S(1)}, bf16[2,256,128]{2,1,0:T(8,128)(2,1)S(1)}, u32[]{:S(2)}, u32[]{:S(2)}) collective-permute-start(bf16[2,256,128]{2,1,0:T(8,128)(2,1)S(1)} %shard_map.62.refs_32_), channel_id=1, source_target_pairs={{8,3},{9,2},{10,7},{11,6},{12,1},{13,0},{14,5},{15,4}} | collective-permute-start | bytes 393224 | tf_op jit(solution)/shard_map/ppermute | solution.py:282
  (22 other events, 155.1 us)
where the time goes:
time: 157 us; the launch traced here: 156 us
  starting transfers between devices  125 us (80%)
  waiting for transfers between devices  15.7 us (10%)
  Pallas kernels  14.6 us (9%)
    ppermute x14, starting transfers between devices, in_layers(): out.append(lax.ppermute(value, axes, pairs))  89.6 us
    ppermute x31, starting transfers between devices, to_layer(): out.append(lax.ppermute(value, axes, pairs))  35.2 us
    pallas_call x5, Pallas kernels, call(): pl.pallas_call(body, out_shape=outs, in_specs=[spec] * len(args), out_spe...  12.9 us
    ppermute x14, waiting for transfers between devices, in_layers(): out.append(lax.ppermute(value, axes, pairs))  9.44 us
    ppermute x31, waiting for transfers between devices, to_layer(): out.append(lax.ppermute(value, axes, pairs))  6.26 us
  transfers between devices with their start and end apart: 45, of which 7 were waited for; matrix products, arithmetic and copies ran while one was open for 0% of the time, Pallas kernels for 4%

commit v1 on v0

--- a/solution.py
+++ b/solution.py
@@ -36,16 +36,16 @@
     "in": (2, 0, 3, 1),
     "own": (0, 1, 2, 3),
 }
+FEED = ("far", "out", "in", "own")
 ORDER = ("far0", "own1", "far1", "out0", "out1", "in0", "in1", "own0")
 
 
 def routes(count):
-    if count == len(ORDER):
-        return [
-            [QUARTERS[slot[:-1]][h // 2] * 2 + (h % 2 ^ int(slot[-1])) for h in range(count)]
-            for slot in ORDER
-        ]
-    return [[(h + s) % count for h in range(count)] for s in range(count - 1, -1, -1)]
+    half = count // 4
+    return [
+        [QUARTERS[slot[:-1]][h // half] * half + (h % half ^ int(slot[-1])) for h in range(count)]
+        for slot in ORDER
+    ]
 
 
 def partner(step, fan):
@@ -117,20 +117,24 @@
     )(*[pltpu.with_memory_space_constraint(a, pltpu.HBM) for a in args])
 
 
-def sort_fields(orders, groups, fan, split):
+def sort_fields(orders, shards, fan):
     harmonics = orders.shape[1]
     blocks = harmonics // LANES
-    pieces = len(groups[0])
 
     def body(orders_ref, *refs):
         shard_refs, out_ref, whole = refs[:-2], refs[-2], refs[-1]
-        values = [r[...] for r in shard_refs[:pieces]]
-        if len(groups) > 1:
-            low = lax.axis_index("layer") < split
-            values = [
-                jnp.where(low, v, r[...]) for v, r in zip(values, shard_refs[pieces:])
-            ]
-        fill(whole, values, fan)
+        if fan:
+            here = lax.axis_index("harm")
+            for name, ref in zip(FEED, shard_refs):
+                quarter = jnp.int32(QUARTERS[name].index(0))
+                for spot in range(1, 4):
+                    quarter = jnp.where(here // 2 == spot, QUARTERS[name].index(spot), quarter)
+                size = ref.shape[2]
+                for part in range(2):
+                    start = (quarter * 2 + (here % 2 ^ part)) * size
+                    put(whole, pl.multiple_of(start, size), ref[part])
+        else:
+            put(whole, 0, shard_refs[0][...])
         targets = orders_ref[...] ^ (LANES - 1)
         chunk = 4 * LANES
 
@@ -153,18 +157,23 @@
     return call(
         body,
         VMEM((2 * LANES, blocks * 2 * LANES), BF16),
-        [orders, *[a for group in groups for a in group]],
+        [orders, *shards],
         24,
         [VMEM((harmonics, 2 * LANES), BF16)],
     )
+
+
+def put(whole, start, value):
+    rows = pl.ds(start, value.shape[1])
+    whole[rows, :LANES] = value[0]
+    whole[rows, LANES:] = value[1]
 
 
 def fill(whole, shards, fan):
     for step, value in enumerate(shards):
         size = value.shape[1]
         start = pl.multiple_of(partner(step, fan) * size, size) if fan else 0
-        whole[pl.ds(start, size), :LANES] = value[0]
-        whole[pl.ds(start, size), LANES:] = value[1]
+        put(whole, start, value)
 
 
 def finish(matrix, orders, factors, sets, belows, fan, band, scale):
@@ -256,7 +265,7 @@
     harmonics = orders.shape[0]
     columns = source.shape[2]
     rows = source.shape[1]
-    fan = rows % LANES == 0 and layers > 3
+    fan = rows % LANES == 0 and count == len(ORDER) and layers > 2
     band = 2 * harmonics // count
     scale = 1.0 / math.sqrt(harmonics * columns)
     axes = ("layer", "harm")
@@ -282,15 +291,9 @@
             out.append(lax.ppermute(value, axes, pairs))
         return out
 
-    def in_layers(value, members):
-        out = []
-        for route in plan:
-            if route == still:
-                out.append(value)
-                continue
-            pairs = [(r * count + h, r * count + route[h]) for r in members for h in range(count)]
-            out.append(lax.ppermute(value, axes, pairs))
-        return out
+    def in_layers(value, route):
+        pairs = [(r * count + h, r * count + route[h]) for r in range(layers) for h in range(count)]
+        return lax.ppermute(value, axes, pairs)
 
     matrix, own, table = bring(transfer[0], source, orders.reshape(1, harmonics))
     if fan:
@@ -302,20 +305,24 @@
         shards[-1] = own
     sets = [shards]
     belows = []
-    early = tuple(r for r in range(layers) if r < layers // 2)
-    late = tuple(r for r in range(layers) if r >= layers // 2)
     mine = []
     for layer in range(top, 0, -1):
         below = propagate(matrix, shards, fan)
         belows.append(below)
         shards = to_layer(below, [layer] * count, layer - 1)
         sets.append(shards)
-        if fan and layer > top - 2:
+        if fan and layer == top:
             held, _ = lax.optimization_barrier((fields[0], below))
-            mine.append(in_layers(held, early if layer == top else late))
+            beside = in_layers(held, [h ^ 1 for h in range(count)])
+        if fan and layer == top - 1:
+            pair, _ = lax.optimization_barrier((jnp.stack([fields[0], beside]), below))
+            for name in FEED[:-1]:
+                turn = QUARTERS[name]
+                mine.append(in_layers(pair, [turn[h // 2] * 2 + h % 2 for h in range(count)]))
+            mine.append(pair)
     if not fan:
-        mine = [gathered(fields[0])]
-    factors = sort_fields(table, mine, fan, len(early))
+        mine = gathered(fields[0])
+    factors = sort_fields(table, mine, fan)
     grads, bottom = finish(
         matrix, table, factors, sets[::-1], belows[::-1], fan, band, scale
     )

time: 157 us -> 103 us (0.66)
  starting transfers between devices: 125 us -> 42.1 us
  waiting for transfers between devices: 15.7 us -> 43.9 us
    ppermute x14 -> x4, starting transfers between devices: 89.6 us -> 6.92 us  [in_layers(): return lax.ppermute(value, axes, pairs)]
    ppermute x31, waiting for transfers between devices: 6.26 us -> 38.6 us  [to_layer(): out.append(lax.ppermute(value, axes, pairs))]
    ppermute x14 -> x4, waiting for transfers between devices: 9.44 us -> 5.39 us  [in_layers(): return lax.ppermute(value, axes, pairs)]
  transfers between devices with their start and end apart: 45 -> 35, of which waited for: 7 -> 6; matrix products, arithmetic and copies ran while one was open for 0% -> 0% of each run, Pallas kernels for 4% -> 6%
where the time goes in v1:
time: 103 us; the launch traced here: 102 us
  waiting for transfers between devices  43.9 us (43%)
  starting transfers between devices  42.1 us (41%)
  Pallas kernels  14.4 us (14%)
  between operations  1.12 us (1%)
    ppermute x31, waiting for transfers between devices, to_layer(): out.append(lax.ppermute(value, axes, pairs))  38.6 us
    ppermute x31, starting transfers between devices, to_layer(): out.append(lax.ppermute(value, axes, pairs))  35.2 us
    pallas_call x5, Pallas kernels, call(): pl.pallas_call(body, out_shape=outs, in_specs=[spec] * len(args), out_spe...  12.8 us
    ppermute x4, starting transfers between devices, in_layers(): return lax.ppermute(value, axes, pairs)  6.92 us
    ppermute x4, waiting for transfers between devices, in_layers(): return lax.ppermute(value, axes, pairs)  5.39 us
  transfers between devices with their start and end apart: 35, of which 6 were waited for; matrix products, arithmetic and copies ran while one was open for 0% of the time, Pallas kernels for 6%

profile of v1, /device:TPU:0, one launch (start us, length us, event | category | flops | bytes accessed | tf_op | source)
XLA Modules:
  0.0 101.6 jit_solution(13743270965922793208)
XLA Ops:
  2.0 9.6 %collective-permute-start.2 = (bf16[2,256,128]{2,1,0:T(8,128)(2,1)}, bf16[2,256,128]{2,1,0:T(8,128)(2,1)S(1)}, u32[]{:S(2)}, u32[]{:S(2)}) collective-permute-start(bf16[2,256,128]{2,1,0:T(8,128)(2,1)} %refs_1_.1), channel_id=1, source_target_pairs={{0,31},{1,30},{2,29},{3,28},{4,27},{5,26},{6,25},{7,24}} | collective-permute-start | bytes 393224 | tf_op jit(solution)/shard_map/ppermute | solution.py:291
  12.9 1.3 %collective-permute-start.5 = (bf16[2,256,128]{2,1,0:T(8,128)(2,1)}, bf16[2,256,128]{2,1,0:T(8,128)(2,1)S(1)}, u32[]{:S(2)}, u32[]{:S(2)}) collective-permute-start(bf16[2,256,128]{2,1,0:T(8,128)(2,1)} %refs_1_.1), channel_id=1, source_target_pairs={{0,28},{1,29},{2,24},{3,25},{4,30},{5,31},{6,26},{7,27}} | collective-permute-start | bytes 393224 | tf_op jit(solution)/shard_map/ppermute | solution.py:291
  14.9 1.6 %bring.1 = (bf16[2,256,2048]{2,1,0:T(8,128)(2,1)S(1)}, bf16[2,256,128]{2,1,0:T(8,128)(2,1)S(1)}, s32[1,2048]{1,0:T(1,128)S(1)}) custom-call(bf16[2,256,2048]{2,1,0:T(8,128)(2,1)} %bitcast.4, bf16[2,256,128]{2,1,0:T(8,128)(2,1)} %refs_1_.1, s32[1,2048]{1,0:T(1,128)} %bitcast.7), custom_call_target="tpu_custom_call" | custom-call | tf_op jit(solution)/shard_map/bring/pallas_call | solution.py:109
  23.3 1.7 %collective-permute-start.7 = (bf16[2,256,128]{2,1,0:T(8,128)(2,1)S(1)}, bf16[2,256,128]{2,1,0:T(8,128)(2,1)S(1)}, u32[]{:S(2)}, u32[]{:S(2)}) collective-permute-start(bf16[2,256,128]{2,1,0:T(8,128)(2,1)S(1)} %bitcast.5), channel_id=1, source_target_pairs={{0,1},{1,0},{2,3},{3,2},{4,5},{5,4},{6,7},{7,6},{8,9},{9,8},{10,11... | collective-permute-start | bytes 393224 | tf_op jit(solution)/shard_map/ppermute | solution.py:296
  25.1 0.7 shard_map.60.refs_33_
  28.5 0.8 collective-permute-done.7
  30.7 2.2 %collective-permute-start.16 = (bf16[2,2,256,128]{3,2,1,0:T(8,128)(2,1)S(1)}, bf16[2,2,256,128]{3,2,1,0:T(8,128)(2,1)S(1)}, u32[]{:S(2)}, u32[]{:S(2)}) collective-permute-start(bf16[2,2,256,128]{3,2,1,0:T(8,128)(2,1)S(1)} %pad_maximum_fusion.refs_3_), channel_id=1, source_target_pairs={{0,6},{1,7},{2,4},{3,5},{4,2},{5,3},{6,0},{7,1},{8,14},{9,15},{10,... | collective-permute-start | bytes 786440 | tf_op jit(solution)/shard_map/ppermute | solution.py:296
  33.0 1.2 %collective-permute-start.17 = (bf16[2,2,256,128]{3,2,1,0:T(8,128)(2,1)S(1)}, bf16[2,2,256,128]{3,2,1,0:T(8,128)(2,1)S(1)}, u32[]{:S(2)}, u32[]{:S(2)}) collective-permute-start(bf16[2,2,256,128]{3,2,1,0:T(8,128)(2,1)S(1)} %pad_maximum_fusion.refs_3_), channel_id=1, source_target_pairs={{0,2},{1,3},{2,6},{3,7},{4,0},{5,1},{6,4},{7,5},{8,10},{9,11},{10,... | collective-permute-start | bytes 786440 | tf_op jit(solution)/shard_map/ppermute | solution.py:296
  34.2 1.7 %collective-permute-start.18 = (bf16[2,2,256,128]{3,2,1,0:T(8,128)(2,1)S(1)}, bf16[2,2,256,128]{3,2,1,0:T(8,128)(2,1)S(1)}, u32[]{:S(2)}, u32[]{:S(2)}) collective-permute-start(bf16[2,2,256,128]{3,2,1,0:T(8,128)(2,1)S(1)} %pad_maximum_fusion.refs_3_), channel_id=1, source_target_pairs={{0,4},{1,5},{2,0},{3,1},{4,6},{5,7},{6,2},{7,3},{8,12},{9,13},{10,... | collective-permute-start | bytes 786440 | tf_op jit(solution)/shard_map/ppermute | solution.py:296
  37.3 0.7 shard_map.62.refs_32_
  38.0 1.3 %collective-permute-start.27 = (bf16[2,256,128]{2,1,0:T(8,128)(2,1)S(1)}, bf16[2,256,128]{2,1,0:T(8,128)(2,1)S(1)}, u32[]{:S(2)}, u32[]{:S(2)}) collective-permute-start(bf16[2,256,128]{2,1,0:T(8,128)(2,1)S(1)} %shard_map.62.refs_32_), channel_id=1, source_target_pairs={{8,6},{9,7},{10,4},{11,5},{12,2},{13,3},{14,0},{15,1}} | collective-permute-start | bytes 393224 | tf_op jit(solution)/shard_map/ppermute | solution.py:291
  39.3 1.3 %collective-permute-start.28 = (bf16[2,256,128]{2,1,0:T(8,128)(2,1)S(1)}, bf16[2,256,128]{2,1,0:T(8,128)(2,1)S(1)}, u32[]{:S(2)}, u32[]{:S(2)}) collective-permute-start(bf16[2,256,128]{2,1,0:T(8,128)(2,1)S(1)} %shard_map.62.refs_32_), channel_id=1, source_target_pairs={{8,1},{9,0},{10,3},{11,2},{12,5},{13,4},{14,7},{15,6}} | collective-permute-start | bytes 393224 | tf_op jit(solution)/shard_map/ppermute | solution.py:291
  40.6 1.3 %collective-permute-start.29 = (bf16[2,256,128]{2,1,0:T(8,128)(2,1)S(1)}, bf16[2,256,128]{2,1,0:T(8,128)(2,1)S(1)}, u32[]{:S(2)}, u32[]{:S(2)}) collective-permute-start(bf16[2,256,128]{2,1,0:T(8,128)(2,1)S(1)} %shard_map.62.refs_32_), channel_id=1, source_target_pairs={{8,7},{9,6},{10,5},{11,4},{12,3},{13,2},{14,1},{15,0}} | collective-permute-start | bytes 393224 | tf_op jit(solution)/shard_map/ppermute | solution.py:291
  41.9 4.5 %collective-permute-done.17.refs_1_ = bf16[2,2,256,128]{3,2,1,0:T(8,128)(2,1)S(1)} collective-permute-done((bf16[2,2,256,128]{3,2,1,0:T(8,128)(2,1)S(1)}, bf16[2,2,256,128]{3,2,1,0:T(8,128)(2,1)S(1)}, u32[]{:S(2)}, u32[]{:S(2)}) %collective-permute-start.17) | collective-permute-done | bytes 262176 | tf_op jit(solution)/shard_map/ppermute | solution.py:296
  46.5 1.3 %collective-permute-start.30 = (bf16[2,256,128]{2,1,0:T(8,128)(2,1)S(1)}, bf16[2,256,128]{2,1,0:T(8,128)(2,1)S(1)}, u32[]{:S(2)}, u32[]{:S(2)}) collective-permute-start(bf16[2,256,128]{2,1,0:T(8,128)(2,1)S(1)} %shard_map.62.refs_32_), channel_id=1, source_target_pairs={{8,2},{9,3},{10,6},{11,7},{12,0},{13,1},{14,4},{15,5}} | collective-permute-start | bytes 393224 | tf_op jit(solution)/shard_map/ppermute | solution.py:291
  47.8 1.3 %collective-permute-start.31 = (bf16[2,256,128]{2,1,0:T(8,128)(2,1)S(1)}, bf16[2,256,128]{2,1,0:T(8,128)(2,1)S(1)}, u32[]{:S(2)}, u32[]{:S(2)}) collective-permute-start(bf16[2,256,128]{2,1,0:T(8,128)(2,1)S(1)} %shard_map.62.refs_32_), channel_id=1, source_target_pairs={{8,3},{9,2},{10,7},{11,6},{12,1},{13,0},{14,5},{15,4}} | collective-permute-start | bytes 393224 | tf_op jit(solution)/shard_map/ppermute | solution.py:291
  49.1 34.0 %collective-permute-done.27.refs_0_ = bf16[2,256,128]{2,1,0:T(8,128)(2,1)S(1)} collective-permute-done((bf16[2,256,128]{2,1,0:T(8,128)(2,1)S(1)}, bf16[2,256,128]{2,1,0:T(8,128)(2,1)S(1)}, u32[]{:S(2)}, u32[]{:S(2)}) %collective-permute-start.27) | collective-permute-done | bytes 131104 | tf_op jit(solution)/shard_map/ppermute | solution.py:291
  83.0 1.3 %collective-permute-start.32 = (bf16[2,256,128]{2,1,0:T(8,128)(2,1)S(1)}, bf16[2,256,128]{2,1,0:T(8,128)(2,1)S(1)}, u32[]{:S(2)}, u32[]{:S(2)}) collective-permute-start(bf16[2,256,128]{2,1,0:T(8,128)(2,1)S(1)} %shard_map.62.refs_32_), channel_id=1, source_target_pairs={{8,4},{9,5},{10,0},{11,1},{12,6},{13,7},{14,2},{15,3}} | collective-permute-start | bytes 393224 | tf_op jit(solution)/shard_map/ppermute | solution.py:291
  84.3 2.6 %collective-permute-done.28.refs_1_ = bf16[2,256,128]{2,1,0:T(8,128)(2,1)S(1)} collective-permute-done((bf16[2,256,128]{2,1,0:T(8,128)(2,1)S(1)}, bf16[2,256,128]{2,1,0:T(8,128)(2,1)S(1)}, u32[]{:S(2)}, u32[]{:S(2)}) %collective-permute-start.28) | collective-permute-done | bytes 131104 | tf_op jit(solution)/shard_map/ppermute | solution.py:291
  86.9 1.3 %collective-permute-start.33 = (bf16[2,256,128]{2,1,0:T(8,128)(2,1)S(1)}, bf16[2,256,128]{2,1,0:T(8,128)(2,1)S(1)}, u32[]{:S(2)}, u32[]{:S(2)}) collective-permute-start(bf16[2,256,128]{2,1,0:T(8,128)(2,1)S(1)} %shard_map.62.refs_32_), channel_id=1, source_target_pairs={{8,5},{9,4},{10,1},{11,0},{12,7},{13,6},{14,3},{15,2}} | collective-permute-start | bytes 393224 | tf_op jit(solution)/shard_map/ppermute | solution.py:291
  88.2 1.3 %collective-permute-start.34 = (bf16[2,256,128]{2,1,0:T(8,128)(2,1)S(1)}, bf16[2,256,128]{2,1,0:T(8,128)(2,1)S(1)}, u32[]{:S(2)}, u32[]{:S(2)}) collective-permute-start(bf16[2,256,128]{2,1,0:T(8,128)(2,1)S(1)} %shard_map.62.refs_32_), channel_id=1, source_target_pairs={{8,0},{9,1},{10,2},{11,3},{12,4},{13,5},{14,6},{15,7}} | collective-permute-start | bytes 393224 | tf_op jit(solution)/shard_map/ppermute | solution.py:291
  89.5 3.2 %shard_map.61.factors_ref = bf16[256,4096]{1,0:T(8,128)(2,1)S(1)} custom-call(s32[1,2048]{1,0:T(1,128)S(1)} %get-tuple-element.8.orders_ref, bf16[2,2,256,128]{3,2,1,0:T(8,128)(2,1)S(1)} %collective-permute-done.16.refs_0_, bf16[2,2,256,128]{3,2,1,0:T(8,128)(2,1)S(1)} %collective-permute-done.17.refs_1_, ...), custom_call_target="tpu_custom_call" | custom-call | tf_op jit(solution)/shard_map/pallas_call | solution.py:19
  92.8 1.4 %collective-permute-done.33.refs_6_ = bf16[2,256,128]{2,1,0:T(8,128)(2,1)S(1)} collective-permute-done((bf16[2,256,128]{2,1,0:T(8,128)(2,1)S(1)}, bf16[2,256,128]{2,1,0:T(8,128)(2,1)S(1)}, u32[]{:S(2)}, u32[]{:S(2)}) %collective-permute-start.33) | collective-permute-done | bytes 131104 | tf_op jit(solution)/shard_map/ppermute | solution.py:291
  94.1 7.5 %shard_map.63 = (f32[1,2,512]{2,1,0:T(2,128)}, bf16[1,2,256,128]{3,2,1,0:T(8,128)(2,1)}) custom-call(bf16[2,256,2048]{2,1,0:T(8,128)(2,1)S(1)} %get-tuple-element.7.matrix_ref, s32[1,2048]{1,0:T(1,128)S(1)} %get-tuple-element.8.orders_ref, bf16[256,4096]{1,0:T(8,128)(2,1)S(1)} %shard_map.61.factors_ref, ...), custom_call_target="tpu_custom_call" | custom-call | tf_op jit(solution)/shard_map/pallas_call | solution.py:19
  (55 shorter events, 15.4 us)
Async XLA Ops:
  0.6 12.3 %collective-permute-start = (bf16[2,256,128]{2,1,0:T(8,128)(2,1)}, bf16[2,256,128]{2,1,0:T(8,128)(2,1)S(1)}, u32[]{:S(2)}, u32[]{:S(2)}) collective-permute-start(bf16[2,256,128]{2,1,0:T(8,128)(2,1)} %refs_1_.1), channel_id=1, source_target_pairs={{8,30},{9,31},{10,28},{11,29},{12,26},{13,27},{14,24},{15,25}} | collective-permute-start | bytes 393224 | tf_op jit(solution)/shard_map/ppermute | solution.py:291
  1.3 12.9 %collective-permute-start.1 = (bf16[2,256,128]{2,1,0:T(8,128)(2,1)}, bf16[2,256,128]{2,1,0:T(8,128)(2,1)S(1)}, u32[]{:S(2)}, u32[]{:S(2)}) collective-permute-start(bf16[2,256,128]{2,1,0:T(8,128)(2,1)} %refs_1_.1), channel_id=1, source_target_pairs={{16,25},{17,24},{18,27},{19,26},{20,29},{21,28},{22,31},{23,30}} | collective-permute-start | bytes 393224 | tf_op jit(solution)/shard_map/ppermute | solution.py:291
  2.0 14.6 %collective-permute-start.2 = (bf16[2,256,128]{2,1,0:T(8,128)(2,1)}, bf16[2,256,128]{2,1,0:T(8,128)(2,1)S(1)}, u32[]{:S(2)}, u32[]{:S(2)}) collective-permute-start(bf16[2,256,128]{2,1,0:T(8,128)(2,1)} %refs_1_.1), channel_id=1, source_target_pairs={{0,31},{1,30},{2,29},{3,28},{4,27},{5,26},{6,25},{7,24}} | collective-permute-start | bytes 393224 | tf_op jit(solution)/shard_map/ppermute | solution.py:291
  11.5 5.0 %collective-permute-start.3 = (bf16[2,256,128]{2,1,0:T(8,128)(2,1)}, bf16[2,256,128]{2,1,0:T(8,128)(2,1)S(1)}, u32[]{:S(2)}, u32[]{:S(2)}) collective-permute-start(bf16[2,256,128]{2,1,0:T(8,128)(2,1)} %refs_1_.1), channel_id=1, source_target_pairs={{8,26},{9,27},{10,30},{11,31},{12,24},{13,25},{14,28},{15,29}} | collective-permute-start | bytes 393224 | tf_op jit(solution)/shard_map/ppermute | solution.py:291
  12.2 4.3 %collective-permute-start.4 = (bf16[2,256,128]{2,1,0:T(8,128)(2,1)}, bf16[2,256,128]{2,1,0:T(8,128)(2,1)S(1)}, u32[]{:S(2)}, u32[]{:S(2)}) collective-permute-start(bf16[2,256,128]{2,1,0:T(8,128)(2,1)} %refs_1_.1), channel_id=1, source_target_pairs={{16,27},{17,26},{18,31},{19,30},{20,25},{21,24},{22,29},{23,28}} | collective-permute-start | bytes 393224 | tf_op jit(solution)/shard_map/ppermute | solution.py:291
  12.9 4.2 %collective-permute-start.5 = (bf16[2,256,128]{2,1,0:T(8,128)(2,1)}, bf16[2,256,128]{2,1,0:T(8,128)(2,1)S(1)}, u32[]{:S(2)}, u32[]{:S(2)}) collective-permute-start(bf16[2,256,128]{2,1,0:T(8,128)(2,1)} %refs_1_.1), channel_id=1, source_target_pairs={{0,28},{1,29},{2,24},{3,25},{4,30},{5,31},{6,26},{7,27}} | collective-permute-start | bytes 393224 | tf_op jit(solution)/shard_map/ppermute | solution.py:291
  20.6 4.5 %collective-permute-start.12 = (bf16[2,256,128]{2,1,0:T(8,128)(2,1)S(1)}, bf16[2,256,128]{2,1,0:T(8,128)(2,1)S(1)}, u32[]{:S(2)}, u32[]{:S(2)}) collective-permute-start(bf16[2,256,128]{2,1,0:T(8,128)(2,1)S(1)} %shard_map.59.refs_34_), channel_id=1, source_target_pairs={{24,19},{25,18},{26,23},{27,22},{28,17},{29,16},{30,21},{31,20}} | collective-permute-start | bytes 393224 | tf_op jit(solution)/shard_map/ppermute | solution.py:291
  23.3 6.0 %collective-permute-start.7 = (bf16[2,256,128]{2,1,0:T(8,128)(2,1)S(1)}, bf16[2,256,128]{2,1,0:T(8,128)(2,1)S(1)}, u32[]{:S(2)}, u32[]{:S(2)}) collective-permute-start(bf16[2,256,128]{2,1,0:T(8,128)(2,1)S(1)} %bitcast.5), channel_id=1, source_target_pairs={{0,1},{1,0},{2,3},{3,2},{4,5},{5,4},{6,7},{7,6},{8,9},{9,8},{10,11... | collective-permute-start | bytes 393224 | tf_op jit(solution)/shard_map/ppermute | solution.py:296
  26.5 4.3 %collective-permute-start.20 = (bf16[2,256,128]{2,1,0:T(8,128)(2,1)S(1)}, bf16[2,256,128]{2,1,0:T(8,128)(2,1)S(1)}, u32[]{:S(2)}, u32[]{:S(2)}) collective-permute-start(bf16[2,256,128]{2,1,0:T(8,128)(2,1)S(1)} %shard_map.60.refs_33_), channel_id=1, source_target_pairs={{16,9},{17,8},{18,11},{19,10},{20,13},{21,12},{22,15},{23,14}} | collective-permute-start | bytes 393224 | tf_op jit(solution)/shard_map/ppermute | solution.py:291
  27.2 5.8 %collective-permute-start.21 = (bf16[2,256,128]{2,1,0:T(8,128)(2,1)S(1)}, bf16[2,256,128]{2,1,0:T(8,128)(2,1)S(1)}, u32[]{:S(2)}, u32[]{:S(2)}) collective-permute-start(bf16[2,256,128]{2,1,0:T(8,128)(2,1)S(1)} %shard_map.60.refs_33_), channel_id=1, source_target_pairs={{16,15},{17,14},{18,13},{19,12},{20,11},{21,10},{22,9},{23,8}} | collective-permute-start | bytes 393224 | tf_op jit(solution)/shard_map/ppermute | solution.py:291
  27.8 6.4 %collective-permute-start.22 = (bf16[2,256,128]{2,1,0:T(8,128)(2,1)S(1)}, bf16[2,256,128]{2,1,0:T(8,128)(2,1)S(1)}, u32[]{:S(2)}, u32[]{:S(2)}) collective-permute-start(bf16[2,256,128]{2,1,0:T(8,128)(2,1)S(1)} %shard_map.60.refs_33_), channel_id=1, source_target_pairs={{16,10},{17,11},{18,14},{19,15},{20,8},{21,9},{22,12},{23,13}} | collective-permute-start | bytes 393224 | tf_op jit(solution)/shard_map/ppermute | solution.py:291
  29.3 6.6 %collective-permute-start.23 = (bf16[2,256,128]{2,1,0:T(8,128)(2,1)S(1)}, bf16[2,256,128]{2,1,0:T(8,128)(2,1)S(1)}, u32[]{:S(2)}, u32[]{:S(2)}) collective-permute-start(bf16[2,256,128]{2,1,0:T(8,128)(2,1)S(1)} %shard_map.60.refs_33_), channel_id=1, source_target_pairs={{16,11},{17,10},{18,15},{19,14},{20,9},{21,8},{22,13},{23,12}} | collective-permute-start | bytes 393224 | tf_op jit(solution)/shard_map/ppermute | solution.py:291
  30.0 6.6 %collective-permute-start.24 = (bf16[2,256,128]{2,1,0:T(8,128)(2,1)S(1)}, bf16[2,256,128]{2,1,0:T(8,128)(2,1)S(1)}, u32[]{:S(2)}, u32[]{:S(2)}) collective-permute-start(bf16[2,256,128]{2,1,0:T(8,128)(2,1)S(1)} %shard_map.60.refs_33_), channel_id=1, source_target_pairs={{16,12},{17,13},{18,8},{19,9},{20,14},{21,15},{22,10},{23,11}} | collective-permute-start | bytes 393224 | tf_op jit(solution)/shard_map/ppermute | solution.py:291
  30.7 9.9 %collective-permute-start.16 = (bf16[2,2,256,128]{3,2,1,0:T(8,128)(2,1)S(1)}, bf16[2,2,256,128]{3,2,1,0:T(8,128)(2,1)S(1)}, u32[]{:S(2)}, u32[]{:S(2)}) collective-permute-start(bf16[2,2,256,128]{3,2,1,0:T(8,128)(2,1)S(1)} %pad_maximum_fusion.refs_3_), channel_id=1, source_target_pairs={{0,6},{1,7},{2,4},{3,5},{4,2},{5,3},{6,0},{7,1},{8,14},{9,15},{10,... | collective-permute-start | bytes 786440 | tf_op jit(solution)/shard_map/ppermute | solution.py:296
  33.0 13.5 %collective-permute-start.17 = (bf16[2,2,256,128]{3,2,1,0:T(8,128)(2,1)S(1)}, bf16[2,2,256,128]{3,2,1,0:T(8,128)(2,1)S(1)}, u32[]{:S(2)}, u32[]{:S(2)}) collective-permute-start(bf16[2,2,256,128]{3,2,1,0:T(8,128)(2,1)S(1)} %pad_maximum_fusion.refs_3_), channel_id=1, source_target_pairs={{0,2},{1,3},{2,6},{3,7},{4,0},{5,1},{6,4},{7,5},{8,10},{9,11},{10,... | collective-permute-start | bytes 786440 | tf_op jit(solution)/shard_map/ppermute | solution.py:296
  34.2 13.5 %collective-permute-start.18 = (bf16[2,2,256,128]{3,2,1,0:T(8,128)(2,1)S(1)}, bf16[2,2,256,128]{3,2,1,0:T(8,128)(2,1)S(1)}, u32[]{:S(2)}, u32[]{:S(2)}) collective-permute-start(bf16[2,2,256,128]{3,2,1,0:T(8,128)(2,1)S(1)} %pad_maximum_fusion.refs_3_), channel_id=1, source_target_pairs={{0,4},{1,5},{2,0},{3,1},{4,6},{5,7},{6,2},{7,3},{8,12},{9,13},{10,... | collective-permute-start | bytes 786440 | tf_op jit(solution)/shard_map/ppermute | solution.py:296
  38.0 45.0 %collective-permute-start.27 = (bf16[2,256,128]{2,1,0:T(8,128)(2,1)S(1)}, bf16[2,256,128]{2,1,0:T(8,128)(2,1)S(1)}, u32[]{:S(2)}, u32[]{:S(2)}) collective-permute-start(bf16[2,256,128]{2,1,0:T(8,128)(2,1)S(1)} %shard_map.62.refs_32_), channel_id=1, source_target_pairs={{8,6},{9,7},{10,4},{11,5},{12,2},{13,3},{14,0},{15,1}} | collective-permute-start | bytes 393224 | tf_op jit(solution)/shard_map/ppermute | solution.py:291
  39.3 47.6 %collective-permute-start.28 = (bf16[2,256,128]{2,1,0:T(8,128)(2,1)S(1)}, bf16[2,256,128]{2,1,0:T(8,128)(2,1)S(1)}, u32[]{:S(2)}, u32[]{:S(2)}) collective-permute-start(bf16[2,256,128]{2,1,0:T(8,128)(2,1)S(1)} %shard_map.62.refs_32_), channel_id=1, source_target_pairs={{8,1},{9,0},{10,3},{11,2},{12,5},{13,4},{14,7},{15,6}} | collective-permute-start | bytes 393224 | tf_op jit(solution)/shard_map/ppermute | solution.py:291
  40.6 47.6 %collective-permute-start.29 = (bf16[2,256,128]{2,1,0:T(8,128)(2,1)S(1)}, bf16[2,256,128]{2,1,0:T(8,128)(2,1)S(1)}, u32[]{:S(2)}, u32[]{:S(2)}) collective-permute-start(bf16[2,256,128]{2,1,0:T(8,128)(2,1)S(1)} %shard_map.62.refs_32_), channel_id=1, source_target_pairs={{8,7},{9,6},{10,5},{11,4},{12,3},{13,2},{14,1},{15,0}} | collective-permute-start | bytes 393224 | tf_op jit(solution)/shard_map/ppermute | solution.py:291
  46.5 46.3 %collective-permute-start.30 = (bf16[2,256,128]{2,1,0:T(8,128)(2,1)S(1)}, bf16[2,256,128]{2,1,0:T(8,128)(2,1)S(1)}, u32[]{:S(2)}, u32[]{:S(2)}) collective-permute-start(bf16[2,256,128]{2,1,0:T(8,128)(2,1)S(1)} %shard_map.62.refs_32_), channel_id=1, source_target_pairs={{8,2},{9,3},{10,6},{11,7},{12,0},{13,1},{14,4},{15,5}} | collective-permute-start | bytes 393224 | tf_op jit(solution)/shard_map/ppermute | solution.py:291
  47.8 45.0 %collective-permute-start.31 = (bf16[2,256,128]{2,1,0:T(8,128)(2,1)S(1)}, bf16[2,256,128]{2,1,0:T(8,128)(2,1)S(1)}, u32[]{:S(2)}, u32[]{:S(2)}) collective-permute-start(bf16[2,256,128]{2,1,0:T(8,128)(2,1)S(1)} %shard_map.62.refs_32_), channel_id=1, source_target_pairs={{8,3},{9,2},{10,7},{11,6},{12,1},{13,0},{14,5},{15,4}} | collective-permute-start | bytes 393224 | tf_op jit(solution)/shard_map/ppermute | solution.py:291
  83.0 9.7 %collective-permute-start.32 = (bf16[2,256,128]{2,1,0:T(8,128)(2,1)S(1)}, bf16[2,256,128]{2,1,0:T(8,128)(2,1)S(1)}, u32[]{:S(2)}, u32[]{:S(2)}) collective-permute-start(bf16[2,256,128]{2,1,0:T(8,128)(2,1)S(1)} %shard_map.62.refs_32_), channel_id=1, source_target_pairs={{8,4},{9,5},{10,0},{11,1},{12,6},{13,7},{14,2},{15,3}} | collective-permute-start | bytes 393224 | tf_op jit(solution)/shard_map/ppermute | solution.py:291
  86.9 7.2 %collective-permute-start.33 = (bf16[2,256,128]{2,1,0:T(8,128)(2,1)S(1)}, bf16[2,256,128]{2,1,0:T(8,128)(2,1)S(1)}, u32[]{:S(2)}, u32[]{:S(2)}) collective-permute-start(bf16[2,256,128]{2,1,0:T(8,128)(2,1)S(1)} %shard_map.62.refs_32_), channel_id=1, source_target_pairs={{8,5},{9,4},{10,1},{11,0},{12,7},{13,6},{14,3},{15,2}} | collective-permute-start | bytes 393224 | tf_op jit(solution)/shard_map/ppermute | solution.py:291
  88.2 5.9 %collective-permute-start.34 = (bf16[2,256,128]{2,1,0:T(8,128)(2,1)S(1)}, bf16[2,256,128]{2,1,0:T(8,128)(2,1)S(1)}, u32[]{:S(2)}, u32[]{:S(2)}) collective-permute-start(bf16[2,256,128]{2,1,0:T(8,128)(2,1)S(1)} %shard_map.62.refs_32_), channel_id=1, source_target_pairs={{8,0},{9,1},{10,2},{11,3},{12,4},{13,5},{14,6},{15,7}} | collective-permute-start | bytes 393224 | tf_op jit(solution)/shard_map/ppermute | solution.py:291
  (12 other events, 39.0 us)

commit v2 on v1

--- a/solution.py
+++ b/solution.py
@@ -117,7 +117,7 @@
     )(*[pltpu.with_memory_space_constraint(a, pltpu.HBM) for a in args])
 
 
-def sort_fields(orders, shards, fan):
+def sort_fields(orders, shards, fan, split):
     harmonics = orders.shape[1]
     blocks = harmonics // LANES
 
@@ -125,14 +125,21 @@
         shard_refs, out_ref, whole = refs[:-2], refs[-2], refs[-1]
         if fan:
             here = lax.axis_index("harm")
-            for name, ref in zip(FEED, shard_refs):
+            low = lax.axis_index("layer") < split
+            moves = len(FEED) - 1
+            for place, name in enumerate(FEED):
                 quarter = jnp.int32(QUARTERS[name].index(0))
                 for spot in range(1, 4):
                     quarter = jnp.where(here // 2 == spot, QUARTERS[name].index(spot), quarter)
-                size = ref.shape[2]
+                size = shard_refs[-1].shape[2]
                 for part in range(2):
+                    value = shard_refs[-1][part]
+                    if place < moves:
+                        value = jnp.where(
+                            low, shard_refs[place][part], shard_refs[moves + place][part]
+                        )
                     start = (quarter * 2 + (here % 2 ^ part)) * size
-                    put(whole, pl.multiple_of(start, size), ref[part])
+                    put(whole, pl.multiple_of(start, size), value)
         else:
             put(whole, 0, shard_refs[0][...])
         targets = orders_ref[...] ^ (LANES - 1)
@@ -291,9 +298,18 @@
             out.append(lax.ppermute(value, axes, pairs))
         return out
 
-    def in_layers(value, route):
-        pairs = [(r * count + h, r * count + route[h]) for r in range(layers) for h in range(count)]
+    def in_layers(value, members, route):
+        pairs = [(r * count + h, r * count + route[h]) for r in members for h in range(count)]
+        if min(members) == 0 and max(members) < top:
+            spare = (max(members) + 1) * count
+            pairs.append((spare, spare))
         return lax.ppermute(value, axes, pairs)
+
+    def along(value, members):
+        return [
+            in_layers(value, members, [QUARTERS[name][h // 2] * 2 + h % 2 for h in range(count)])
+            for name in FEED[:-1]
+        ]
 
     matrix, own, table = bring(transfer[0], source, orders.reshape(1, harmonics))
     if fan:
@@ -301,8 +317,10 @@
     else:
         origins = [top]
     shards = to_layer(source, origins, top)
+    split = layers // 2
     if fan:
         shards[-1] = own
+        beside = in_layers(fields[0], range(layers), [h ^ 1 for h in range(count)])
     sets = [shards]
     belows = []
     mine = []
@@ -312,17 +330,16 @@
         shards = to_layer(below, [layer] * count, layer - 1)
         sets.append(shards)
         if fan and layer == top:
-            held, _ = lax.optimization_barrier((fields[0], below))
-            beside = in_layers(held, [h ^ 1 for h in range(count)])
+            beside, _ = lax.optimization_barrier((beside, below))
+            pair = jnp.stack([fields[0], beside])
+            mine += along(pair, range(split))
         if fan and layer == top - 1:
-            pair, _ = lax.optimization_barrier((jnp.stack([fields[0], beside]), below))
-            for name in FEED[:-1]:
-                turn = QUARTERS[name]
-                mine.append(in_layers(pair, [turn[h // 2] * 2 + h % 2 for h in range(count)]))
-            mine.append(pair)
+            held, _ = lax.optimization_barrier((pair, below))
+            mine += along(held, range(split, layers))
+            mine.append(held)
     if not fan:
         mine = gathered(fields[0])
-    factors = sort_fields(table, mine, fan)
+    factors = sort_fields(table, mine, fan, split)
     grads, bottom = finish(
         matrix, table, factors, sets[::-1], belows[::-1], fan, band, scale
     )

time: 103 us -> 103 us (level)
  starting transfers between devices: 42.1 us -> 66.4 us
  waiting for transfers between devices: 43.9 us -> 20.2 us
    ppermute x31, waiting for transfers between devices: 38.6 us -> 5.49 us  [to_layer(): out.append(lax.ppermute(value, axes, pairs))]
    ppermute x4 -> x7, starting transfers between devices: 6.92 us -> 31.2 us  [in_layers(): return lax.ppermute(value, axes, pairs)]
    ppermute x4 -> x7, waiting for transfers between devices: 5.39 us -> 14.7 us  [in_layers(): return lax.ppermute(value, axes, pairs)]
  transfers between devices with their start and end apart: 35 -> 38, of which waited for: 6 -> 6; matrix products, arithmetic and copies ran while one was open for 0% -> 0% of each run, Pallas kernels for 6% -> 7%
where the time goes in v2:
time: 103 us; the launch traced here: 102 us
  starting transfers between devices  66.4 us (64%)
  waiting for transfers between devices  20.2 us (20%)
  Pallas kernels  14.5 us (14%)
  between operations  1.24 us (1%)
    ppermute x31, starting transfers between devices, to_layer(): out.append(lax.ppermute(value, axes, pairs))  35.2 us
    ppermute x7, starting transfers between devices, in_layers(): return lax.ppermute(value, axes, pairs)  31.2 us
    ppermute x7, waiting for transfers between devices, in_layers(): return lax.ppermute(value, axes, pairs)  14.7 us
    pallas_call x5, Pallas kernels, call(): pl.pallas_call(body, out_shape=outs, in_specs=[spec] * len(args), out_spe...  12.9 us
    ppermute x31, waiting for transfers between devices, to_layer(): out.append(lax.ppermute(value, axes, pairs))  5.49 us
  transfers between devices with their start and end apart: 38, of which 6 were waited for; matrix products, arithmetic and copies ran while one was open for 0% of the time, Pallas kernels for 7%

profile of v2, /device:TPU:0, one launch (start us, length us, event | category | flops | bytes accessed | tf_op | source)
XLA Modules:
  0.0 102.4 jit_solution(6912244352737344302)
XLA Ops:
  2.0 9.6 %collective-permute-start.3 = (bf16[2,256,128]{2,1,0:T(8,128)(2,1)}, bf16[2,256,128]{2,1,0:T(8,128)(2,1)S(1)}, u32[]{:S(2)}, u32[]{:S(2)}) collective-permute-start(bf16[2,256,128]{2,1,0:T(8,128)(2,1)} %refs_1_.1), channel_id=1, source_target_pairs={{0,31},{1,30},{2,29},{3,28},{4,27},{5,26},{6,25},{7,24}} | collective-permute-start | bytes 393224 | tf_op jit(solution)/shard_map/ppermute | solution.py:298
  12.9 1.3 %collective-permute-start.6 = (bf16[2,256,128]{2,1,0:T(8,128)(2,1)}, bf16[2,256,128]{2,1,0:T(8,128)(2,1)S(1)}, u32[]{:S(2)}, u32[]{:S(2)}) collective-permute-start(bf16[2,256,128]{2,1,0:T(8,128)(2,1)} %refs_1_.1), channel_id=1, source_target_pairs={{0,28},{1,29},{2,24},{3,25},{4,30},{5,31},{6,26},{7,27}} | collective-permute-start | bytes 393224 | tf_op jit(solution)/shard_map/ppermute | solution.py:298
  14.9 5.8 %collective-permute-start = (bf16[2,256,128]{2,1,0:T(8,128)(2,1)}, bf16[2,256,128]{2,1,0:T(8,128)(2,1)S(1)}, u32[]{:S(2)}, u32[]{:S(2)}) collective-permute-start(bf16[2,256,128]{2,1,0:T(8,128)(2,1)} %bitcast.5), channel_id=1, source_target_pairs={{0,1},{1,0},{2,3},{3,2},{4,5},{5,4},{6,7},{7,6},{8,9},{9,8},{10,11... | collective-permute-start | bytes 393224 | tf_op jit(solution)/shard_map/ppermute | solution.py:306
  20.7 1.6 %bring.1 = (bf16[2,256,2048]{2,1,0:T(8,128)(2,1)S(1)}, bf16[2,256,128]{2,1,0:T(8,128)(2,1)S(1)}, s32[1,2048]{1,0:T(1,128)S(1)}) custom-call(bf16[2,256,2048]{2,1,0:T(8,128)(2,1)} %bitcast.4, bf16[2,256,128]{2,1,0:T(8,128)(2,1)} %refs_1_.1, s32[1,2048]{1,0:T(1,128)} %bitcast.7), custom_call_target="tpu_custom_call" | custom-call | tf_op jit(solution)/shard_map/bring/pallas_call | solution.py:109
  22.4 0.7 shard_map.59.refs_34_
  25.8 0.8 collective-permute-done
  29.4 14.5 %collective-permute-start.8 = (bf16[2,2,256,128]{3,2,1,0:T(8,128)(2,1)S(1)}, bf16[2,2,256,128]{3,2,1,0:T(8,128)(2,1)S(1)}, u32[]{:S(2)}, u32[]{:S(2)}) collective-permute-start(bf16[2,2,256,128]{3,2,1,0:T(8,128)(2,1)S(1)} %pad_maximum_fusion.refs_6_), channel_id=1, source_target_pairs={{0,6},{1,7},{2,4},{3,5},{4,2},{5,3},{6,0},{7,1},{8,14},{9,15},{10,... | collective-permute-start | bytes 786440 | tf_op jit(solution)/shard_map/ppermute | solution.py:306
  43.9 0.7 shard_map.60.refs_33_
  47.3 6.9 %collective-permute-done.8.refs_0_ = bf16[2,2,256,128]{3,2,1,0:T(8,128)(2,1)S(1)} collective-permute-done((bf16[2,2,256,128]{3,2,1,0:T(8,128)(2,1)S(1)}, bf16[2,2,256,128]{3,2,1,0:T(8,128)(2,1)S(1)}, u32[]{:S(2)}, u32[]{:S(2)}) %collective-permute-start.8) | collective-permute-done | bytes 262176 | tf_op jit(solution)/shard_map/ppermute | solution.py:306
  57.0 7.0 %collective-permute-start.9 = (bf16[2,2,256,128]{3,2,1,0:T(8,128)(2,1)S(1)}, bf16[2,2,256,128]{3,2,1,0:T(8,128)(2,1)S(1)}, u32[]{:S(2)}, u32[]{:S(2)}) collective-permute-start(bf16[2,2,256,128]{3,2,1,0:T(8,128)(2,1)S(1)} %pad_maximum_fusion.refs_6_), channel_id=1, source_target_pairs={{0,2},{1,3},{2,6},{3,7},{4,0},{5,1},{6,4},{7,5},{8,10},{9,11},{10,... | collective-permute-start | bytes 786440 | tf_op jit(solution)/shard_map/ppermute | solution.py:306
  64.0 1.9 %collective-permute-start.10 = (bf16[2,2,256,128]{3,2,1,0:T(8,128)(2,1)S(1)}, bf16[2,2,256,128]{3,2,1,0:T(8,128)(2,1)S(1)}, u32[]{:S(2)}, u32[]{:S(2)}) collective-permute-start(bf16[2,2,256,128]{3,2,1,0:T(8,128)(2,1)S(1)} %pad_maximum_fusion.refs_6_), channel_id=1, source_target_pairs={{0,4},{1,5},{2,0},{3,1},{4,6},{5,7},{6,2},{7,3},{8,12},{9,13},{10,... | collective-permute-start | bytes 786440 | tf_op jit(solution)/shard_map/ppermute | solution.py:306
  69.4 1.3 %collective-permute-start.30 = (bf16[2,256,128]{2,1,0:T(8,128)(2,1)S(1)}, bf16[2,256,128]{2,1,0:T(8,128)(2,1)S(1)}, u32[]{:S(2)}, u32[]{:S(2)}) collective-permute-start(bf16[2,256,128]{2,1,0:T(8,128)(2,1)S(1)} %shard_map.62.refs_32_), channel_id=1, source_target_pairs={{8,6},{9,7},{10,4},{11,5},{12,2},{13,3},{14,0},{15,1}} | collective-permute-start | bytes 393224 | tf_op jit(solution)/shard_map/ppermute | solution.py:298
  70.7 6.4 %collective-permute-done.10.refs_2_ = bf16[2,2,256,128]{3,2,1,0:T(8,128)(2,1)S(1)} collective-permute-done((bf16[2,2,256,128]{3,2,1,0:T(8,128)(2,1)S(1)}, bf16[2,2,256,128]{3,2,1,0:T(8,128)(2,1)S(1)}, u32[]{:S(2)}, u32[]{:S(2)}) %collective-permute-start.10) | collective-permute-done | bytes 262176 | tf_op jit(solution)/shard_map/ppermute | solution.py:306
  77.1 1.3 %collective-permute-start.31 = (bf16[2,256,128]{2,1,0:T(8,128)(2,1)S(1)}, bf16[2,256,128]{2,1,0:T(8,128)(2,1)S(1)}, u32[]{:S(2)}, u32[]{:S(2)}) collective-permute-start(bf16[2,256,128]{2,1,0:T(8,128)(2,1)S(1)} %shard_map.62.refs_32_), channel_id=1, source_target_pairs={{8,1},{9,0},{10,3},{11,2},{12,5},{13,4},{14,7},{15,6}} | collective-permute-start | bytes 393224 | tf_op jit(solution)/shard_map/ppermute | solution.py:298
  78.4 1.3 %collective-permute-start.32 = (bf16[2,256,128]{2,1,0:T(8,128)(2,1)S(1)}, bf16[2,256,128]{2,1,0:T(8,128)(2,1)S(1)}, u32[]{:S(2)}, u32[]{:S(2)}) collective-permute-start(bf16[2,256,128]{2,1,0:T(8,128)(2,1)S(1)} %shard_map.62.refs_32_), channel_id=1, source_target_pairs={{8,7},{9,6},{10,5},{11,4},{12,3},{13,2},{14,1},{15,0}} | collective-permute-start | bytes 393224 | tf_op jit(solution)/shard_map/ppermute | solution.py:298
  79.7 1.3 %collective-permute-start.33 = (bf16[2,256,128]{2,1,0:T(8,128)(2,1)S(1)}, bf16[2,256,128]{2,1,0:T(8,128)(2,1)S(1)}, u32[]{:S(2)}, u32[]{:S(2)}) collective-permute-start(bf16[2,256,128]{2,1,0:T(8,128)(2,1)S(1)} %shard_map.62.refs_32_), channel_id=1, source_target_pairs={{8,2},{9,3},{10,6},{11,7},{12,0},{13,1},{14,4},{15,5}} | collective-permute-start | bytes 393224 | tf_op jit(solution)/shard_map/ppermute | solution.py:298
  81.0 1.3 %collective-permute-start.34 = (bf16[2,256,128]{2,1,0:T(8,128)(2,1)S(1)}, bf16[2,256,128]{2,1,0:T(8,128)(2,1)S(1)}, u32[]{:S(2)}, u32[]{:S(2)}) collective-permute-start(bf16[2,256,128]{2,1,0:T(8,128)(2,1)S(1)} %shard_map.62.refs_32_), channel_id=1, source_target_pairs={{8,3},{9,2},{10,7},{11,6},{12,1},{13,0},{14,5},{15,4}} | collective-permute-start | bytes 393224 | tf_op jit(solution)/shard_map/ppermute | solution.py:298
  82.3 1.3 %collective-permute-start.35 = (bf16[2,256,128]{2,1,0:T(8,128)(2,1)S(1)}, bf16[2,256,128]{2,1,0:T(8,128)(2,1)S(1)}, u32[]{:S(2)}, u32[]{:S(2)}) collective-permute-start(bf16[2,256,128]{2,1,0:T(8,128)(2,1)S(1)} %shard_map.62.refs_32_), channel_id=1, source_target_pairs={{8,4},{9,5},{10,0},{11,1},{12,6},{13,7},{14,2},{15,3}} | collective-permute-start | bytes 393224 | tf_op jit(solution)/shard_map/ppermute | solution.py:298
  83.6 4.1 %collective-permute-done.31.refs_1_ = bf16[2,256,128]{2,1,0:T(8,128)(2,1)S(1)} collective-permute-done((bf16[2,256,128]{2,1,0:T(8,128)(2,1)S(1)}, bf16[2,256,128]{2,1,0:T(8,128)(2,1)S(1)}, u32[]{:S(2)}, u32[]{:S(2)}) %collective-permute-start.31) | collective-permute-done | bytes 131104 | tf_op jit(solution)/shard_map/ppermute | solution.py:298
  87.7 1.3 %collective-permute-start.36 = (bf16[2,256,128]{2,1,0:T(8,128)(2,1)S(1)}, bf16[2,256,128]{2,1,0:T(8,128)(2,1)S(1)}, u32[]{:S(2)}, u32[]{:S(2)}) collective-permute-start(bf16[2,256,128]{2,1,0:T(8,128)(2,1)S(1)} %shard_map.62.refs_32_), channel_id=1, source_target_pairs={{8,5},{9,4},{10,1},{11,0},{12,7},{13,6},{14,3},{15,2}} | collective-permute-start | bytes 393224 | tf_op jit(solution)/shard_map/ppermute | solution.py:298
  89.0 1.3 %collective-permute-start.37 = (bf16[2,256,128]{2,1,0:T(8,128)(2,1)S(1)}, bf16[2,256,128]{2,1,0:T(8,128)(2,1)S(1)}, u32[]{:S(2)}, u32[]{:S(2)}) collective-permute-start(bf16[2,256,128]{2,1,0:T(8,128)(2,1)S(1)} %shard_map.62.refs_32_), channel_id=1, source_target_pairs={{8,0},{9,1},{10,2},{11,3},{12,4},{13,5},{14,6},{15,7}} | collective-permute-start | bytes 393224 | tf_op jit(solution)/shard_map/ppermute | solution.py:298
  90.3 3.3 %shard_map.61.factors_ref = bf16[256,4096]{1,0:T(8,128)(2,1)S(1)} custom-call(s32[1,2048]{1,0:T(1,128)S(1)} %get-tuple-element.8.orders_ref, bf16[2,2,256,128]{3,2,1,0:T(8,128)(2,1)S(1)} %collective-permute-done.8.refs_0_, bf16[2,2,256,128]{3,2,1,0:T(8,128)(2,1)S(1)} %collective-permute-done.9.refs_1_, ...), custom_call_target="tpu_custom_call" | custom-call | tf_op jit(solution)/shard_map/pallas_call | solution.py:19
  93.6 1.3 %collective-permute-done.36.refs_6_ = bf16[2,256,128]{2,1,0:T(8,128)(2,1)S(1)} collective-permute-done((bf16[2,256,128]{2,1,0:T(8,128)(2,1)S(1)}, bf16[2,256,128]{2,1,0:T(8,128)(2,1)S(1)}, u32[]{:S(2)}, u32[]{:S(2)}) %collective-permute-start.36) | collective-permute-done | bytes 131104 | tf_op jit(solution)/shard_map/ppermute | solution.py:298
  94.9 7.5 %shard_map.63 = (f32[1,2,512]{2,1,0:T(2,128)}, bf16[1,2,256,128]{3,2,1,0:T(8,128)(2,1)}) custom-call(bf16[2,256,2048]{2,1,0:T(8,128)(2,1)S(1)} %get-tuple-element.7.matrix_ref, s32[1,2048]{1,0:T(1,128)S(1)} %get-tuple-element.8.orders_ref, bf16[256,4096]{1,0:T(8,128)(2,1)S(1)} %shard_map.61.factors_ref, ...), custom_call_target="tpu_custom_call" | custom-call | tf_op jit(solution)/shard_map/pallas_call | solution.py:19
  (61 shorter events, 17.5 us)
Async XLA Ops:
  0.6 12.3 %collective-permute-start.1 = (bf16[2,256,128]{2,1,0:T(8,128)(2,1)}, bf16[2,256,128]{2,1,0:T(8,128)(2,1)S(1)}, u32[]{:S(2)}, u32[]{:S(2)}) collective-permute-start(bf16[2,256,128]{2,1,0:T(8,128)(2,1)} %refs_1_.1), channel_id=1, source_target_pairs={{8,30},{9,31},{10,28},{11,29},{12,26},{13,27},{14,24},{15,25}} | collective-permute-start | bytes 393224 | tf_op jit(solution)/shard_map/ppermute | solution.py:298
  1.3 12.9 %collective-permute-start.2 = (bf16[2,256,128]{2,1,0:T(8,128)(2,1)}, bf16[2,256,128]{2,1,0:T(8,128)(2,1)S(1)}, u32[]{:S(2)}, u32[]{:S(2)}) collective-permute-start(bf16[2,256,128]{2,1,0:T(8,128)(2,1)} %refs_1_.1), channel_id=1, source_target_pairs={{16,25},{17,24},{18,27},{19,26},{20,29},{21,28},{22,31},{23,30}} | collective-permute-start | bytes 393224 | tf_op jit(solution)/shard_map/ppermute | solution.py:298
  2.0 12.9 %collective-permute-start.3 = (bf16[2,256,128]{2,1,0:T(8,128)(2,1)}, bf16[2,256,128]{2,1,0:T(8,128)(2,1)S(1)}, u32[]{:S(2)}, u32[]{:S(2)}) collective-permute-start(bf16[2,256,128]{2,1,0:T(8,128)(2,1)} %refs_1_.1), channel_id=1, source_target_pairs={{0,31},{1,30},{2,29},{3,28},{4,27},{5,26},{6,25},{7,24}} | collective-permute-start | bytes 393224 | tf_op jit(solution)/shard_map/ppermute | solution.py:298
  11.5 10.8 %collective-permute-start.4 = (bf16[2,256,128]{2,1,0:T(8,128)(2,1)}, bf16[2,256,128]{2,1,0:T(8,128)(2,1)S(1)}, u32[]{:S(2)}, u32[]{:S(2)}) collective-permute-start(bf16[2,256,128]{2,1,0:T(8,128)(2,1)} %refs_1_.1), channel_id=1, source_target_pairs={{8,26},{9,27},{10,30},{11,31},{12,24},{13,25},{14,28},{15,29}} | collective-permute-start | bytes 393224 | tf_op jit(solution)/shard_map/ppermute | solution.py:298
  14.9 11.7 %collective-permute-start = (bf16[2,256,128]{2,1,0:T(8,128)(2,1)}, bf16[2,256,128]{2,1,0:T(8,128)(2,1)S(1)}, u32[]{:S(2)}, u32[]{:S(2)}) collective-permute-start(bf16[2,256,128]{2,1,0:T(8,128)(2,1)} %bitcast.5), channel_id=1, source_target_pairs={{0,1},{1,0},{2,3},{3,2},{4,5},{5,4},{6,7},{7,6},{8,9},{9,8},{10,11... | collective-permute-start | bytes 393224 | tf_op jit(solution)/shard_map/ppermute | solution.py:306
  26.6 17.3 %collective-permute-start.15 = (bf16[2,256,128]{2,1,0:T(8,128)(2,1)S(1)}, bf16[2,256,128]{2,1,0:T(8,128)(2,1)S(1)}, u32[]{:S(2)}, u32[]{:S(2)}) collective-permute-start(bf16[2,256,128]{2,1,0:T(8,128)(2,1)S(1)} %shard_map.59.refs_34_), channel_id=1, source_target_pairs={{24,19},{25,18},{26,23},{27,22},{28,17},{29,16},{30,21},{31,20}} | collective-permute-start | bytes 393224 | tf_op jit(solution)/shard_map/ppermute | solution.py:298
  27.3 16.5 %collective-permute-start.16 = (bf16[2,256,128]{2,1,0:T(8,128)(2,1)S(1)}, bf16[2,256,128]{2,1,0:T(8,128)(2,1)S(1)}, u32[]{:S(2)}, u32[]{:S(2)}) collective-permute-start(bf16[2,256,128]{2,1,0:T(8,128)(2,1)S(1)} %shard_map.59.refs_34_), channel_id=1, source_target_pairs={{24,20},{25,21},{26,16},{27,17},{28,22},{29,23},{30,18},{31,19}} | collective-permute-start | bytes 393224 | tf_op jit(solution)/shard_map/ppermute | solution.py:298
  28.0 15.9 %collective-permute-start.17 = (bf16[2,256,128]{2,1,0:T(8,128)(2,1)S(1)}, bf16[2,256,128]{2,1,0:T(8,128)(2,1)S(1)}, u32[]{:S(2)}, u32[]{:S(2)}) collective-permute-start(bf16[2,256,128]{2,1,0:T(8,128)(2,1)S(1)} %shard_map.59.refs_34_), channel_id=1, source_target_pairs={{24,21},{25,20},{26,17},{27,16},{28,23},{29,22},{30,19},{31,18}} | collective-permute-start | bytes 393224 | tf_op jit(solution)/shard_map/ppermute | solution.py:298
  28.7 15.2 %collective-permute-start.18 = (bf16[2,256,128]{2,1,0:T(8,128)(2,1)S(1)}, bf16[2,256,128]{2,1,0:T(8,128)(2,1)S(1)}, u32[]{:S(2)}, u32[]{:S(2)}) collective-permute-start(bf16[2,256,128]{2,1,0:T(8,128)(2,1)S(1)} %shard_map.59.refs_34_), channel_id=1, source_target_pairs={{24,16},{25,17},{26,18},{27,19},{28,20},{29,21},{30,22},{31,23}} | collective-permute-start | bytes 393224 | tf_op jit(solution)/shard_map/ppermute | solution.py:298
  29.4 24.9 %collective-permute-start.8 = (bf16[2,2,256,128]{3,2,1,0:T(8,128)(2,1)S(1)}, bf16[2,2,256,128]{3,2,1,0:T(8,128)(2,1)S(1)}, u32[]{:S(2)}, u32[]{:S(2)}) collective-permute-start(bf16[2,2,256,128]{3,2,1,0:T(8,128)(2,1)S(1)} %pad_maximum_fusion.refs_6_), channel_id=1, source_target_pairs={{0,6},{1,7},{2,4},{3,5},{4,2},{5,3},{6,0},{7,1},{8,14},{9,15},{10,... | collective-permute-start | bytes 786440 | tf_op jit(solution)/shard_map/ppermute | solution.py:306
  54.9 11.0 %collective-permute-start.27 = (bf16[2,256,128]{2,1,0:T(8,128)(2,1)S(1)}, bf16[2,256,128]{2,1,0:T(8,128)(2,1)S(1)}, u32[]{:S(2)}, u32[]{:S(2)}) collective-permute-start(bf16[2,256,128]{2,1,0:T(8,128)(2,1)S(1)} %shard_map.60.refs_33_), channel_id=1, source_target_pairs={{16,12},{17,13},{18,8},{19,9},{20,14},{21,15},{22,10},{23,11}} | collective-permute-start | bytes 393224 | tf_op jit(solution)/shard_map/ppermute | solution.py:298
  55.6 11.1 %collective-permute-start.28 = (bf16[2,256,128]{2,1,0:T(8,128)(2,1)S(1)}, bf16[2,256,128]{2,1,0:T(8,128)(2,1)S(1)}, u32[]{:S(2)}, u32[]{:S(2)}) collective-permute-start(bf16[2,256,128]{2,1,0:T(8,128)(2,1)S(1)} %shard_map.60.refs_33_), channel_id=1, source_target_pairs={{16,13},{17,12},{18,9},{19,8},{20,15},{21,14},{22,11},{23,10}} | collective-permute-start | bytes 393224 | tf_op jit(solution)/shard_map/ppermute | solution.py:298
  56.3 11.1 %collective-permute-start.29 = (bf16[2,256,128]{2,1,0:T(8,128)(2,1)S(1)}, bf16[2,256,128]{2,1,0:T(8,128)(2,1)S(1)}, u32[]{:S(2)}, u32[]{:S(2)}) collective-permute-start(bf16[2,256,128]{2,1,0:T(8,128)(2,1)S(1)} %shard_map.60.refs_33_), channel_id=1, source_target_pairs={{16,8},{17,9},{18,10},{19,11},{20,12},{21,13},{22,14},{23,15}} | collective-permute-start | bytes 393224 | tf_op jit(solution)/shard_map/ppermute | solution.py:298
  57.0 12.4 %collective-permute-start.9 = (bf16[2,2,256,128]{3,2,1,0:T(8,128)(2,1)S(1)}, bf16[2,2,256,128]{3,2,1,0:T(8,128)(2,1)S(1)}, u32[]{:S(2)}, u32[]{:S(2)}) collective-permute-start(bf16[2,2,256,128]{3,2,1,0:T(8,128)(2,1)S(1)} %pad_maximum_fusion.refs_6_), channel_id=1, source_target_pairs={{0,2},{1,3},{2,6},{3,7},{4,0},{5,1},{6,4},{7,5},{8,10},{9,11},{10,... | collective-permute-start | bytes 786440 | tf_op jit(solution)/shard_map/ppermute | solution.py:306
  64.0 13.0 %collective-permute-start.10 = (bf16[2,2,256,128]{3,2,1,0:T(8,128)(2,1)S(1)}, bf16[2,2,256,128]{3,2,1,0:T(8,128)(2,1)S(1)}, u32[]{:S(2)}, u32[]{:S(2)}) collective-permute-start(bf16[2,2,256,128]{3,2,1,0:T(8,128)(2,1)S(1)} %pad_maximum_fusion.refs_6_), channel_id=1, source_target_pairs={{0,4},{1,5},{2,0},{3,1},{4,6},{5,7},{6,2},{7,3},{8,12},{9,13},{10,... | collective-permute-start | bytes 786440 | tf_op jit(solution)/shard_map/ppermute | solution.py:306
  66.0 12.4 %collective-permute-start.19 = (bf16[2,2,256,128]{3,2,1,0:T(8,128)(2,1)S(1)}, bf16[2,2,256,128]{3,2,1,0:T(8,128)(2,1)S(1)}, u32[]{:S(2)}, u32[]{:S(2)}) collective-permute-start(bf16[2,2,256,128]{3,2,1,0:T(8,128)(2,1)S(1)} %pad_maximum_fusion.refs_6_), channel_id=1, source_target_pairs={{16,22},{17,23},{18,20},{19,21},{20,18},{21,19},{22,16},{23,17},{2... | collective-permute-start | bytes 786440 | tf_op jit(solution)/shard_map/ppermute | solution.py:306
  66.7 13.0 %collective-permute-start.20 = (bf16[2,2,256,128]{3,2,1,0:T(8,128)(2,1)S(1)}, bf16[2,2,256,128]{3,2,1,0:T(8,128)(2,1)S(1)}, u32[]{:S(2)}, u32[]{:S(2)}) collective-permute-start(bf16[2,2,256,128]{3,2,1,0:T(8,128)(2,1)S(1)} %pad_maximum_fusion.refs_6_), channel_id=1, source_target_pairs={{16,18},{17,19},{18,22},{19,23},{20,16},{21,17},{22,20},{23,21},{2... | collective-permute-start | bytes 786440 | tf_op jit(solution)/shard_map/ppermute | solution.py:306
  67.4 13.6 %collective-permute-start.21 = (bf16[2,2,256,128]{3,2,1,0:T(8,128)(2,1)S(1)}, bf16[2,2,256,128]{3,2,1,0:T(8,128)(2,1)S(1)}, u32[]{:S(2)}, u32[]{:S(2)}) collective-permute-start(bf16[2,2,256,128]{3,2,1,0:T(8,128)(2,1)S(1)} %pad_maximum_fusion.refs_6_), channel_id=1, source_target_pairs={{16,20},{17,21},{18,16},{19,17},{20,22},{21,23},{22,18},{23,19},{2... | collective-permute-start | bytes 786440 | tf_op jit(solution)/shard_map/ppermute | solution.py:306
  69.4 12.9 %collective-permute-start.30 = (bf16[2,256,128]{2,1,0:T(8,128)(2,1)S(1)}, bf16[2,256,128]{2,1,0:T(8,128)(2,1)S(1)}, u32[]{:S(2)}, u32[]{:S(2)}) collective-permute-start(bf16[2,256,128]{2,1,0:T(8,128)(2,1)S(1)} %shard_map.62.refs_32_), channel_id=1, source_target_pairs={{8,6},{9,7},{10,4},{11,5},{12,2},{13,3},{14,0},{15,1}} | collective-permute-start | bytes 393224 | tf_op jit(solution)/shard_map/ppermute | solution.py:298
  77.1 10.7 %collective-permute-start.31 = (bf16[2,256,128]{2,1,0:T(8,128)(2,1)S(1)}, bf16[2,256,128]{2,1,0:T(8,128)(2,1)S(1)}, u32[]{:S(2)}, u32[]{:S(2)}) collective-permute-start(bf16[2,256,128]{2,1,0:T(8,128)(2,1)S(1)} %shard_map.62.refs_32_), channel_id=1, source_target_pairs={{8,1},{9,0},{10,3},{11,2},{12,5},{13,4},{14,7},{15,6}} | collective-permute-start | bytes 393224 | tf_op jit(solution)/shard_map/ppermute | solution.py:298
  78.4 10.7 %collective-permute-start.32 = (bf16[2,256,128]{2,1,0:T(8,128)(2,1)S(1)}, bf16[2,256,128]{2,1,0:T(8,128)(2,1)S(1)}, u32[]{:S(2)}, u32[]{:S(2)}) collective-permute-start(bf16[2,256,128]{2,1,0:T(8,128)(2,1)S(1)} %shard_map.62.refs_32_), channel_id=1, source_target_pairs={{8,7},{9,6},{10,5},{11,4},{12,3},{13,2},{14,1},{15,0}} | collective-permute-start | bytes 393224 | tf_op jit(solution)/shard_map/ppermute | solution.py:298
  79.7 13.9 %collective-permute-start.33 = (bf16[2,256,128]{2,1,0:T(8,128)(2,1)S(1)}, bf16[2,256,128]{2,1,0:T(8,128)(2,1)S(1)}, u32[]{:S(2)}, u32[]{:S(2)}) collective-permute-start(bf16[2,256,128]{2,1,0:T(8,128)(2,1)S(1)} %shard_map.62.refs_32_), channel_id=1, source_target_pairs={{8,2},{9,3},{10,6},{11,7},{12,0},{13,1},{14,4},{15,5}} | collective-permute-start | bytes 393224 | tf_op jit(solution)/shard_map/ppermute | solution.py:298
  81.0 12.6 %collective-permute-start.34 = (bf16[2,256,128]{2,1,0:T(8,128)(2,1)S(1)}, bf16[2,256,128]{2,1,0:T(8,128)(2,1)S(1)}, u32[]{:S(2)}, u32[]{:S(2)}) collective-permute-start(bf16[2,256,128]{2,1,0:T(8,128)(2,1)S(1)} %shard_map.62.refs_32_), channel_id=1, source_target_pairs={{8,3},{9,2},{10,7},{11,6},{12,1},{13,0},{14,5},{15,4}} | collective-permute-start | bytes 393224 | tf_op jit(solution)/shard_map/ppermute | solution.py:298
  82.3 11.3 %collective-permute-start.35 = (bf16[2,256,128]{2,1,0:T(8,128)(2,1)S(1)}, bf16[2,256,128]{2,1,0:T(8,128)(2,1)S(1)}, u32[]{:S(2)}, u32[]{:S(2)}) collective-permute-start(bf16[2,256,128]{2,1,0:T(8,128)(2,1)S(1)} %shard_map.62.refs_32_), channel_id=1, source_target_pairs={{8,4},{9,5},{10,0},{11,1},{12,6},{13,7},{14,2},{15,3}} | collective-permute-start | bytes 393224 | tf_op jit(solution)/shard_map/ppermute | solution.py:298
  (15 other events, 113.7 us)
